TPU v7x, 32 devices: a whole 2x2x4 slice. The times are simulated.
32 devices in a mesh: gx: 4 (over y, core), gy: 8 (over z, x).
Axes of the slice: x: 2, y: 2, z: 4, core: 2. Of those that a mesh axis runs over, the one named last changes fastest.
Arguments:
- thermal_anomaly: float32 [64, 256, 1024], P(None, 'gx', 'gy'), may hold values from -6 to 6
- eastward_shift_ratio: float32 [64, 256, 1024], P(None, 'gx', 'gy'), may hold values from -0.6 to 0.6
- northward_shift_ratio: float32 [64, 256, 1024], P(None, 'gx', 'gy'), may hold values from -0.6 to 0.6
- upward_shift_ratio: float32 [64, 256, 1024], P(None, 'gx', 'gy'), may hold values from -0.6 to 0.6
- emitted_power: float32 [16, 65536], P(None, ('gx', 'gy')), may hold values from 0.2 to 1
- albedo_values: float32 [16, 65536], P(None, ('gx', 'gy')), may hold values from 0.1 to 0.8
- visibility_matrices: bfloat16 [32, 32, 2, 128, 128], P(('gx', 'gy')), may hold values from 0 to 1
- active_pairing_totals: int32 [32, 32], P(('gx', 'gy')), may hold values from 1 to 2, as said below
- sender_panel_group: int32 [32, 32, 2], P(('gx', 'gy')), may hold values from 0 to 15
- receiver_panel_group: int32 [32, 32, 2], P(None, ('gx', 'gy')), may hold values from 0 to 15
- nearest_ground_index: int32 [65536], P(('gx', 'gy')), may hold values from 0 to 11519
Outputs:
- renewed_thermal_anomaly: float32 [64, 256, 1024], P(None, 'gx', 'gy')
- leaving_power: float32 [16, 65536], P(None, ('gx', 'gy'))
Inputs may be any that keep to these rules, and one draw needn't show every extreme that they name: `active_pairing_totals`: in every draw some receiving devices get 2 live slots from every sending device. `sender_panel_group`: A local block index of the sending device. `receiver_panel_group`: A local block index of the receiving device; slots that are not live may hold any index. `nearest_ground_index`: index (x * 144 + y) in the owner's block of cells widened by 8 cells on each side.
All inputs are finite; a program needn't handle non-finite values.
Results may differ from a plain program's by a relative error of at most 0.0003.
Values sent between devices are 32-bit elements; how exact they have to be, the bound alone decides.
No kernel may reach another device: no remote copies, remote signals or barrier semaphores. Data moves between devices by JAX's collectives and lax.ppermute only.
A program may use at most 128 MiB of HBM per device.

v0:
```python
import jax
import jax.numpy as jnp
from jax import lax
from jax.sharding import PartitionSpec as P

MARGIN = 8


heat_gain = 0.02


def with_halo(cells, sides, width):
    for axis, dim in sides:
        count = lax.axis_size(axis)
        head = lax.slice_in_dim(cells, 0, width, axis=dim)
        tail = lax.slice_in_dim(cells, cells.shape[dim] - width, cells.shape[dim], axis=dim)
        cells = jnp.concatenate(
            [
                lax.ppermute(tail, axis, [(i, (i + 1) % count) for i in range(count)]),
                cells,
                lax.ppermute(head, axis, [((i + 1) % count, i) for i in range(count)]),
            ],
            axis=dim,
        )
    return cells


def upwind(behind_two, behind_one, center, ahead_one, ahead_two, velocity):
    rising = (behind_two - 6.0 * behind_one + 3.0 * center + 2.0 * ahead_one) / 6.0
    falling = (-2.0 * behind_one - 3.0 * center + 6.0 * ahead_one - ahead_two) / 6.0
    return jnp.where(velocity >= 0.0, rising, falling)


def vertical(transported_quantity, velocity):
    levels = transported_quantity.shape[0]
    padded = jnp.pad(transported_quantity, ((2, 2), (0, 0), (0, 0)), mode="edge")
    return upwind(
        padded[0:levels],
        padded[1 : levels + 1],
        padded[2 : levels + 2],
        padded[3 : levels + 3],
        padded[4 : levels + 4],
        velocity,
    )


def thermal_change_speed(
    transported_quantity, eastward_shift_ratio, northward_shift_ratio, upward_shift_ratio
):
    extended = with_halo(transported_quantity, (("gx", 1), ("gy", 2)), 2)
    eastward_extent = transported_quantity.shape[1]
    northward_extent = transported_quantity.shape[2]
    strip_x = extended[:, :, 2 : northward_extent + 2]
    strip_y = extended[:, 2 : eastward_extent + 2, :]
    along_x = upwind(
        strip_x[:, 0:eastward_extent],
        strip_x[:, 1 : eastward_extent + 1],
        strip_x[:, 2 : eastward_extent + 2],
        strip_x[:, 3 : eastward_extent + 3],
        strip_x[:, 4 : eastward_extent + 4],
        eastward_shift_ratio,
    )
    along_y = upwind(
        strip_y[:, :, 0:northward_extent],
        strip_y[:, :, 1 : northward_extent + 1],
        strip_y[:, :, 2 : northward_extent + 2],
        strip_y[:, :, 3 : northward_extent + 3],
        strip_y[:, :, 4 : northward_extent + 4],
        northward_shift_ratio,
    )
    return -(
        eastward_shift_ratio * along_x
        + northward_shift_ratio * along_y
        + upward_shift_ratio * vertical(transported_quantity, upward_shift_ratio)
    )


def irradiance(light, blocks, live, source, target):
    bands = light.shape[0]
    width = blocks.shape[-1]
    owned = light.astype(jnp.bfloat16).reshape(bands, -1, width)
    chosen = jnp.take(owned, source, axis=1)
    sent = jnp.einsum("krci,rcij->rckj", chosen, blocks, preferred_element_type=jnp.float32)
    sent = sent * (0.5 / width) * live[:, :, None, None]
    arrived = lax.all_to_all(sent, ("gx", "gy"), split_axis=0, concat_axis=0, tiled=True)
    slots = (target[:, :, None] == jnp.arange(owned.shape[1])[None, None, :]).astype(jnp.float32)
    summed = jnp.einsum("scf,sckj->kfj", slots, arrived, precision=lax.Precision.HIGHEST)
    return summed.reshape(bands, -1)


def fold_margin(extended, margin, along):
    total = extended.shape[along]
    inside = total - 4 * margin
    middle = lax.slice_in_dim(extended, 2 * margin, 2 * margin + inside, axis=along)
    lower_rim = lax.slice_in_dim(extended, 0, margin, axis=along)
    upper_rim = lax.slice_in_dim(extended, total - margin, total, axis=along)
    low_pad = [(0, 0), (0, 0)]
    high_pad = [(0, 0), (0, 0)]
    low_pad[along] = (0, inside - margin)
    high_pad[along] = (inside - margin, 0)
    return middle + jnp.pad(lower_rim, low_pad) + jnp.pad(upper_rim, high_pad)


def on_device(
    thermal_anomaly,
    eastward_shift_ratio,
    northward_shift_ratio,
    upward_shift_ratio,
    emitted_power,
    albedo_values,
    visibility_matrices,
    active_pairing_totals,
    sender_panel_group,
    receiver_panel_group,
    nearest_ground_index,
):
    capacity = sender_panel_group.shape[-1]
    live = (jnp.arange(capacity)[None, :] < active_pairing_totals[0][:, None]).astype(jnp.float32)
    blocks = visibility_matrices[0]
    source = sender_panel_group[0]
    target = receiver_panel_group[:, 0, :]
    first_light = irradiance(emitted_power, blocks, live, source, target)
    bounced = emitted_power + albedo_values * first_light
    second_light = irradiance(bounced, blocks, live, source, target)
    leaving_power = emitted_power + albedo_values * second_light
    absorbed = heat_gain * jnp.sum((1.0 - albedo_values) * second_light, axis=0)
    eastward_extent = thermal_anomaly.shape[1]
    northward_extent = thermal_anomaly.shape[2]
    span_x = eastward_extent + 2 * MARGIN
    span_y = northward_extent + 2 * MARGIN
    ground_energy_transfer = jax.ops.segment_sum(
        absorbed, nearest_ground_index, num_segments=span_x * span_y
    ).reshape(span_x, span_y)
    extended = with_halo(ground_energy_transfer, (("gx", 0), ("gy", 1)), MARGIN)
    wall_warming = fold_margin(fold_margin(extended, MARGIN, 0), MARGIN, 1)
    initial_reflected_share = (
        thermal_anomaly
        + thermal_change_speed(
            thermal_anomaly, eastward_shift_ratio, northward_shift_ratio, upward_shift_ratio
        )
        / 3.0
    )
    repeated_reflected_share = (
        thermal_anomaly
        + thermal_change_speed(
            initial_reflected_share, eastward_shift_ratio, northward_shift_ratio, upward_shift_ratio
        )
        / 2.0
    )
    advanced_thermal_state = thermal_anomaly + thermal_change_speed(
        repeated_reflected_share, eastward_shift_ratio, northward_shift_ratio, upward_shift_ratio
    )
    renewed_thermal_anomaly = advanced_thermal_state.at[0].add(wall_warming)
    return (renewed_thermal_anomaly, leaving_power)


def solution(mesh):
    in_specs = (
        P(None, "gx", "gy"),
        P(None, "gx", "gy"),
        P(None, "gx", "gy"),
        P(None, "gx", "gy"),
        P(None, ("gx", "gy")),
        P(None, ("gx", "gy")),
        P(("gx", "gy"), None, None, None, None),
        P(("gx", "gy"), None),
        P(("gx", "gy"), None, None),
        P(None, ("gx", "gy"), None),
        P(("gx", "gy")),
    )
    out_specs = (P(None, "gx", "gy"), P(None, ("gx", "gy")))
    return jax.shard_map(
        on_device, mesh=mesh, in_specs=in_specs, out_specs=out_specs, check_vma=False
    )
```

profile of v0, /device:TPU:1, one launch (start us, length us, event | category | flops | bytes accessed | tf_op | source)
XLA Modules:
  0.0 186.9 jit_solution(9933536439710815969)
XLA Ops:
  1.9 2.7 %collective-permute-start = (f32[64,2,128]{2,1,0:T(2,128)S(1)}, f32[64,2,128]{2,1,0:T(2,128)S(1)}, u32[]{:S(2)}, u32[]{:S(2)}) collective-permute-start(f32[64,2,128]{2,1,0:T(2,128)S(1)} %get-tuple-element.30), channel_id=1, source_target_pairs={{0,8},{8,16},{16,24},{24,0},{1,9},{9,17},{17,25},{25,1},{2,10},{10... | collective-permute-start | bytes 196616 | tf_op jit(solution)/shard_map/ppermute | solution.py:19
  10.1 5.6 %all-to-all-start = ((f32[32,2,16,128]{3,2,1,0:T(8,128)}), f32[32,2,16,128]{3,2,1,0:T(8,128)S(1)}, u32[]{:S(2)}, u32[]{:S(2)}) async-start(f32[32,2,16,128]{3,2,1,0:T(8,128)} %fusion.106), calls=%async_computation | async-start | bytes 1048576 | tf_op jit(solution)/shard_map/all_to_all | solution.py:85
  16.5 3.3 %constant_dynamic-update-slice_fusion.1 = f32[64,66,128]{2,1,0:T(8,128)} fusion(f32[64,64,128]{2,1,0:T(8,128)} %param.15), kind=kLoop, calls=%fused_computation.233 | loop fusion | bytes 4194304
  20.2 2.9 %fusion.148 = (f32[64,68,2]{2,1,0:T(8,128)}, f32[64,68,2]{2,1,0:T(8,128)}) fusion(f32[64,68,128]{2,1,0:T(8,128)S(1)} %pad_maximum_fusion), kind=kLoop, calls=%fused_computation.247 | loop fusion | bytes 139264 | tf_op jit(solution)/shard_map/slice | solution.py:16
  23.1 2.5 %copy.29 = f32[64,68,2]{1,0,2:T(8,128)S(1)} copy(f32[64,68,2]{2,1,0:T(8,128)} %get-tuple-element.19) | data formatting | bytes 69632 | tf_op jit(solution)/shard_map/slice | solution.py:16
  26.9 2.5 %copy.31 = f32[64,68,2]{1,0,2:T(8,128)S(1)} copy(f32[64,68,2]{2,1,0:T(8,128)} %get-tuple-element.20) | data formatting | bytes 69632 | tf_op jit(solution)/shard_map/slice | solution.py:15
  29.4 2.8 %collective-permute-start.3 = (f32[64,68,2]{1,0,2:T(8,128)S(1)}, f32[64,68,2]{1,0,2:T(8,128)S(1)}, u32[]{:S(2)}, u32[]{:S(2)}) collective-permute-start(f32[64,68,2]{1,0,2:T(8,128)S(1)} %copy.31), channel_id=1, source_target_pairs={{1,0},{2,1},{3,2},{4,3},{5,4},{6,5},{7,6},{0,7},{9,8},{10,9},{11,1... | collective-permute-start | bytes 104456 | tf_op jit(solution)/shard_map/ppermute | solution.py:21
  37.5 22.8 %fusion.34 = f32[64,64,128]{2,1,0:T(8,128)S(1)} fusion(f32[64,64,128]{2,1,0:T(8,128)} %param.15, f32[64,64,128]{2,1,0:T(8,128)} %param.18, f32[2,64,128]{2,1,0:T(8,128)S(1)} %reshape.127, f32[64,64,128]{2,1,0:T(8,128)} %param.16, f32[64,2,128]{2,1,0:T(2,128)S(1)} %collective-permute-done, f32[64,64,128]{2,1,0:T(8,128)} %param.17, ...), kind=kLoop, calls=%fused_computation.62 | loop fusion | flops 36175872 | bytes 15011840 | tf_op jit(solution)/shard_map/add | solution.py:137
  63.9 2.4 %collective-permute-done.5 = f32[64,2,128]{2,1,0:T(2,128)S(1)} collective-permute-done((f32[64,2,128]{2,1,0:T(2,128)S(1)}, f32[64,2,128]{2,1,0:T(2,128)S(1)}, u32[]{:S(2)}, u32[]{:S(2)}) %collective-permute-start.5) | collective-permute-done | bytes 65568 | tf_op jit(solution)/shard_map/ppermute | solution.py:21
  66.6 2.9 %fusion.147 = (f32[64,68,2]{2,1,0:T(8,128)}, f32[64,68,2]{2,1,0:T(8,128)}) fusion(f32[64,68,128]{2,1,0:T(8,128)S(1)} %pad_maximum_fusion.1), kind=kLoop, calls=%fused_computation.246 | loop fusion | bytes 139264 | tf_op jit(solution)/shard_map/slice | solution.py:16
  69.5 2.5 %copy.33 = f32[64,68,2]{1,0,2:T(8,128)S(1)} copy(f32[64,68,2]{2,1,0:T(8,128)} %get-tuple-element.17) | data formatting | bytes 69632 | tf_op jit(solution)/shard_map/slice | solution.py:16
  72.1 2.5 %copy.35 = f32[64,68,2]{1,0,2:T(8,128)S(1)} copy(f32[64,68,2]{2,1,0:T(8,128)} %get-tuple-element.18) | data formatting | bytes 69632 | tf_op jit(solution)/shard_map/slice | solution.py:15
  74.6 4.1 %collective-permute-start.7 = (f32[64,68,2]{1,0,2:T(8,128)S(1)}, f32[64,68,2]{1,0,2:T(8,128)S(1)}, u32[]{:S(2)}, u32[]{:S(2)}) collective-permute-start(f32[64,68,2]{1,0,2:T(8,128)S(1)} %copy.35), channel_id=1, source_target_pairs={{1,0},{2,1},{3,2},{4,3},{5,4},{6,5},{7,6},{0,7},{9,8},{10,9},{11,1... | collective-permute-start | bytes 104456 | tf_op jit(solution)/shard_map/ppermute | solution.py:21
  86.8 4.5 %all-to-all-start.1 = ((f32[32,2,16,128]{3,2,1,0:T(8,128)}), f32[32,2,16,128]{3,2,1,0:T(8,128)S(1)}, u32[]{:S(2)}, u32[]{:S(2)}) async-start(f32[32,2,16,128]{3,2,1,0:T(8,128)} %fusion.109), calls=%async_computation.1 | async-start | bytes 1048576 | tf_op jit(solution)/shard_map/all_to_all | solution.py:85
  91.4 24.8 %fusion.22 = f32[64,64,128]{2,1,0:T(8,128)S(1)} fusion(f32[64,64,128]{2,1,0:T(8,128)} %param.15, f32[64,64,128]{2,1,0:T(8,128)} %param.18, f32[2,64,128]{2,1,0:T(8,128)S(1)} %reshape.129, f32[64,64,128]{2,1,0:T(8,128)} %copy-done.3, f32[64,64,128]{2,1,0:T(8,128)} %param.16, f32[64,2,128]{2,1,0:T(2,128)S(1)} %collective-permute-done.4, ...), kind=kLoop, calls=%fused_computation.50 | loop fusion | flops 37224448 | bytes 12914688 | tf_op jit(solution)/shard_map/add | solution.py:144
  119.3 2.4 %collective-permute-done.9 = f32[64,2,128]{2,1,0:T(2,128)S(1)} collective-permute-done((f32[64,2,128]{2,1,0:T(2,128)S(1)}, f32[64,2,128]{2,1,0:T(2,128)S(1)}, u32[]{:S(2)}, u32[]{:S(2)}) %collective-permute-start.9) | collective-permute-done | bytes 65568 | tf_op jit(solution)/shard_map/ppermute | solution.py:21
  122.0 2.9 %fusion.146 = (f32[64,68,2]{2,1,0:T(8,128)}, f32[64,68,2]{2,1,0:T(8,128)}) fusion(f32[64,68,128]{2,1,0:T(8,128)S(1)} %pad_maximum_fusion.2), kind=kLoop, calls=%fused_computation.245 | loop fusion | bytes 139264 | tf_op jit(solution)/shard_map/slice | solution.py:16
  124.9 2.5 %copy.37 = f32[64,68,2]{1,0,2:T(8,128)S(1)} copy(f32[64,68,2]{2,1,0:T(8,128)} %get-tuple-element.15) | data formatting | bytes 69632 | tf_op jit(solution)/shard_map/slice | solution.py:16
  128.6 2.5 %copy.39 = f32[64,68,2]{1,0,2:T(8,128)S(1)} copy(f32[64,68,2]{2,1,0:T(8,128)} %get-tuple-element.16) | data formatting | bytes 69632 | tf_op jit(solution)/shard_map/slice | solution.py:15
  131.0 3.0 %collective-permute-start.11 = (f32[64,68,2]{1,0,2:T(8,128)S(1)}, f32[64,68,2]{1,0,2:T(8,128)S(1)}, u32[]{:S(2)}, u32[]{:S(2)}) collective-permute-start(f32[64,68,2]{1,0,2:T(8,128)S(1)} %copy.39), channel_id=1, source_target_pairs={{1,0},{2,1},{3,2},{4,3},{5,4},{6,5},{7,6},{0,7},{9,8},{10,9},{11,1... | collective-permute-start | bytes 104456 | tf_op jit(solution)/shard_map/ppermute | solution.py:21
  135.4 11.4 %scatter_custom_fusion = f32[11520]{0:T(1024)S(1)} fusion(s32[2048]{0:T(1024)} %param.25, f32[2048]{0:T(1024)S(1)} %broadcast_multiply_fusion, f32[]{:T(128)} %constant.71.clone.1), kind=kCustom, calls=%fused_computation.226 | custom fusion | flops 2048 | bytes 46592 | tf_op jit(solution)/shard_map/scatter-add | solution.py:131
  153.1 3.0 %collective-permute-done.13 = f32[8,144]{1,0:T(8,128)S(1)} collective-permute-done((f32[8,144]{1,0:T(8,128)S(1)}, f32[8,144]{1,0:T(8,128)S(1)}, u32[]{:S(2)}, u32[]{:S(2)}) %collective-permute-start.13) | collective-permute-done | bytes 4640 | tf_op jit(solution)/shard_map/ppermute | solution.py:21
  156.2 4.2 %collective-permute-start.15 = (f32[96,8]{1,0:T(8,128)S(1)}, f32[96,8]{1,0:T(8,128)S(1)}, u32[]{:S(2)}, u32[]{:S(2)}) collective-permute-start(f32[96,8]{1,0:T(8,128)S(1)} %get-tuple-element.36), channel_id=1, source_target_pairs={{1,0},{2,1},{3,2},{4,3},{5,4},{6,5},{7,6},{0,7},{9,8},{10,9},{11,1... | collective-permute-start | bytes 9224 | tf_op jit(solution)/shard_map/ppermute | solution.py:21
  160.4 24.8 %fusion.10 = f32[64,64,128]{2,1,0:T(8,128)S(1)} fusion(f32[64,64,128]{2,1,0:T(8,128)} %param.15, f32[64,64,128]{2,1,0:T(8,128)} %param.18, f32[2,64,128]{2,1,0:T(8,128)S(1)} %reshape.131, f32[64,64,128]{2,1,0:T(8,128)} %copy-done.2, f32[64,64,128]{2,1,0:T(8,128)} %param.16, f32[64,2,128]{2,1,0:T(2,128)S(1)} %collective-permute-done.8, ...), kind=kLoop, calls=%fused_computation.38 | loop fusion | flops 36700160 | bytes 12914688 | tf_op jit(solution)/shard_map/add | solution.py:150
  (97 shorter events, 40.9 us)
Async XLA Ops:
  0.6 7.9 %copy-start = (bf16[1,32,2,128,128]{4,3,2,1,0:T(8,128)(2,1)S(1)}, bf16[1,32,2,128,128]{4,3,2,1,0:T(8,128)(2,1)}, u32[]{:S(2)}) copy-start(bf16[1,32,2,128,128]{4,3,2,1,0:T(8,128)(2,1)} %param.21) | copy-start | bytes 6291460
  1.9 17.9 %collective-permute-start.1 = (f32[64,2,128]{2,1,0:T(2,128)S(1)}, f32[64,2,128]{2,1,0:T(2,128)S(1)}, u32[]{:S(2)}, u32[]{:S(2)}) collective-permute-start(f32[64,2,128]{2,1,0:T(2,128)S(1)} %get-tuple-element.29), channel_id=1, source_target_pairs={{8,0},{16,8},{24,16},{0,24},{9,1},{17,9},{25,17},{1,25},{10,2},{18... | collective-permute-start | bytes 196616 | tf_op jit(solution)/shard_map/ppermute | solution.py:21
  1.9 17.9 %collective-permute-start = (f32[64,2,128]{2,1,0:T(2,128)S(1)}, f32[64,2,128]{2,1,0:T(2,128)S(1)}, u32[]{:S(2)}, u32[]{:S(2)}) collective-permute-start(f32[64,2,128]{2,1,0:T(2,128)S(1)} %get-tuple-element.30), channel_id=1, source_target_pairs={{0,8},{8,16},{16,24},{24,0},{1,9},{9,17},{17,25},{25,1},{2,10},{10... | collective-permute-start | bytes 196616 | tf_op jit(solution)/shard_map/ppermute | solution.py:19
  10.1 73.9 %all-to-all-start = ((f32[32,2,16,128]{3,2,1,0:T(8,128)}), f32[32,2,16,128]{3,2,1,0:T(8,128)S(1)}, u32[]{:S(2)}, u32[]{:S(2)}) async-start(f32[32,2,16,128]{3,2,1,0:T(8,128)} %fusion.106), calls=%async_computation | async-start | bytes 1048576 | tf_op jit(solution)/shard_map/all_to_all | solution.py:85
  25.6 7.3 %collective-permute-start.2 = (f32[64,68,2]{1,0,2:T(8,128)S(1)}, f32[64,68,2]{1,0,2:T(8,128)S(1)}, u32[]{:S(2)}, u32[]{:S(2)}) collective-permute-start(f32[64,68,2]{1,0,2:T(8,128)S(1)} %copy.29), channel_id=1, source_target_pairs={{0,1},{1,2},{2,3},{3,4},{4,5},{5,6},{6,7},{7,0},{8,9},{9,10},{10,1... | collective-permute-start | bytes 104456 | tf_op jit(solution)/shard_map/ppermute | solution.py:19
  29.4 5.8 %collective-permute-start.3 = (f32[64,68,2]{1,0,2:T(8,128)S(1)}, f32[64,68,2]{1,0,2:T(8,128)S(1)}, u32[]{:S(2)}, u32[]{:S(2)}) collective-permute-start(f32[64,68,2]{1,0,2:T(8,128)S(1)} %copy.31), channel_id=1, source_target_pairs={{1,0},{2,1},{3,2},{4,3},{5,4},{6,5},{7,6},{0,7},{9,8},{10,9},{11,1... | collective-permute-start | bytes 104456 | tf_op jit(solution)/shard_map/ppermute | solution.py:21
  60.2 6.4 %copy-start.3 = (f32[64,64,128]{2,1,0:T(8,128)}, f32[64,64,128]{2,1,0:T(8,128)S(1)}, u32[]{:S(2)}) copy-start(f32[64,64,128]{2,1,0:T(8,128)S(1)} %fusion.34) | copy-start | bytes 6291460
  60.3 3.6 %collective-permute-start.4 = (f32[64,2,128]{2,1,0:T(2,128)S(1)}, f32[64,2,128]{2,1,0:T(2,128)S(1)}, u32[]{:S(2)}, u32[]{:S(2)}) collective-permute-start(f32[64,2,128]{2,1,0:T(2,128)S(1)} %get-tuple-element.26), channel_id=1, source_target_pairs={{0,8},{8,16},{16,24},{24,0},{1,9},{9,17},{17,25},{25,1},{2,10},{10... | collective-permute-start | bytes 196616 | tf_op jit(solution)/shard_map/ppermute | solution.py:19
  62.6 3.7 %collective-permute-start.5 = (f32[64,2,128]{2,1,0:T(2,128)S(1)}, f32[64,2,128]{2,1,0:T(2,128)S(1)}, u32[]{:S(2)}, u32[]{:S(2)}) collective-permute-start(f32[64,2,128]{2,1,0:T(2,128)S(1)} %get-tuple-element.25), channel_id=1, source_target_pairs={{8,0},{16,8},{24,16},{0,24},{9,1},{17,9},{25,17},{1,25},{10,2},{18... | collective-permute-start | bytes 196616 | tf_op jit(solution)/shard_map/ppermute | solution.py:21
  72.0 7.5 %collective-permute-start.6 = (f32[64,68,2]{1,0,2:T(8,128)S(1)}, f32[64,68,2]{1,0,2:T(8,128)S(1)}, u32[]{:S(2)}, u32[]{:S(2)}) collective-permute-start(f32[64,68,2]{1,0,2:T(8,128)S(1)} %copy.33), channel_id=1, source_target_pairs={{0,1},{1,2},{2,3},{3,4},{4,5},{5,6},{6,7},{7,0},{8,9},{9,10},{10,1... | collective-permute-start | bytes 104456 | tf_op jit(solution)/shard_map/ppermute | solution.py:19
  74.6 7.1 %collective-permute-start.7 = (f32[64,68,2]{1,0,2:T(8,128)S(1)}, f32[64,68,2]{1,0,2:T(8,128)S(1)}, u32[]{:S(2)}, u32[]{:S(2)}) collective-permute-start(f32[64,68,2]{1,0,2:T(8,128)S(1)} %copy.35), channel_id=1, source_target_pairs={{1,0},{2,1},{3,2},{4,3},{5,4},{6,5},{7,6},{0,7},{9,8},{10,9},{11,1... | collective-permute-start | bytes 104456 | tf_op jit(solution)/shard_map/ppermute | solution.py:21
  79.4 4.6 %copy-start.7 = (s32[32,1,2]{0,2,1:T(2,128)S(1)}, s32[32,1,2]{0,2,1:T(2,128)}, u32[]{:S(2)}) copy-start(s32[32,1,2]{0,2,1:T(2,128)} %param.24) | copy-start | bytes 772
  86.8 47.2 %all-to-all-start.1 = ((f32[32,2,16,128]{3,2,1,0:T(8,128)}), f32[32,2,16,128]{3,2,1,0:T(8,128)S(1)}, u32[]{:S(2)}, u32[]{:S(2)}) async-start(f32[32,2,16,128]{3,2,1,0:T(8,128)} %fusion.109), calls=%async_computation.1 | async-start | bytes 1048576 | tf_op jit(solution)/shard_map/all_to_all | solution.py:85
  116.2 5.8 %copy-start.2 = (f32[64,64,128]{2,1,0:T(8,128)}, f32[64,64,128]{2,1,0:T(8,128)S(1)}, u32[]{:S(2)}) copy-start(f32[64,64,128]{2,1,0:T(8,128)S(1)} %fusion.22) | copy-start | bytes 6291460
  116.3 3.0 %collective-permute-start.8 = (f32[64,2,128]{2,1,0:T(2,128)S(1)}, f32[64,2,128]{2,1,0:T(2,128)S(1)}, u32[]{:S(2)}, u32[]{:S(2)}) collective-permute-start(f32[64,2,128]{2,1,0:T(2,128)S(1)} %get-tuple-element.22), channel_id=1, source_target_pairs={{0,8},{8,16},{16,24},{24,0},{1,9},{9,17},{17,25},{25,1},{2,10},{10... | collective-permute-start | bytes 196616 | tf_op jit(solution)/shard_map/ppermute | solution.py:19
  117.9 3.7 %collective-permute-start.9 = (f32[64,2,128]{2,1,0:T(2,128)S(1)}, f32[64,2,128]{2,1,0:T(2,128)S(1)}, u32[]{:S(2)}, u32[]{:S(2)}) collective-permute-start(f32[64,2,128]{2,1,0:T(2,128)S(1)} %get-tuple-element.21), channel_id=1, source_target_pairs={{8,0},{16,8},{24,16},{0,24},{9,1},{17,9},{25,17},{1,25},{10,2},{18... | collective-permute-start | bytes 196616 | tf_op jit(solution)/shard_map/ppermute | solution.py:21
  127.4 20.9 %collective-permute-start.10 = (f32[64,68,2]{1,0,2:T(8,128)S(1)}, f32[64,68,2]{1,0,2:T(8,128)S(1)}, u32[]{:S(2)}, u32[]{:S(2)}) collective-permute-start(f32[64,68,2]{1,0,2:T(8,128)S(1)} %copy.37), channel_id=1, source_target_pairs={{0,1},{1,2},{2,3},{3,4},{4,5},{5,6},{6,7},{7,0},{8,9},{9,10},{10,1... | collective-permute-start | bytes 104456 | tf_op jit(solution)/shard_map/ppermute | solution.py:19
  131.0 19.5 %collective-permute-start.11 = (f32[64,68,2]{1,0,2:T(8,128)S(1)}, f32[64,68,2]{1,0,2:T(8,128)S(1)}, u32[]{:S(2)}, u32[]{:S(2)}) collective-permute-start(f32[64,68,2]{1,0,2:T(8,128)S(1)} %copy.39), channel_id=1, source_target_pairs={{1,0},{2,1},{3,2},{4,3},{5,4},{6,5},{7,6},{0,7},{9,8},{10,9},{11,1... | collective-permute-start | bytes 104456 | tf_op jit(solution)/shard_map/ppermute | solution.py:21
  146.8 6.2 %collective-permute-start.12 = (f32[8,144]{1,0:T(8,128)S(1)}, f32[8,144]{1,0:T(8,128)S(1)}, u32[]{:S(2)}, u32[]{:S(2)}) collective-permute-start(f32[8,144]{1,0:T(8,128)S(1)} %slice.377), channel_id=1, source_target_pairs={{0,8},{8,16},{16,24},{24,0},{1,9},{9,17},{17,25},{25,1},{2,10},{10... | collective-permute-start | bytes 13832 | tf_op jit(solution)/shard_map/ppermute | solution.py:19
  153.0 3.1 %collective-permute-start.13 = (f32[8,144]{1,0:T(8,128)S(1)}, f32[8,144]{1,0:T(8,128)S(1)}, u32[]{:S(2)}, u32[]{:S(2)}) collective-permute-start(f32[8,144]{1,0:T(8,128)S(1)} %slice.379), channel_id=1, source_target_pairs={{8,0},{16,8},{24,16},{0,24},{9,1},{17,9},{25,17},{1,25},{10,2},{18... | collective-permute-start | bytes 13832 | tf_op jit(solution)/shard_map/ppermute | solution.py:21
  156.2 29.0 %collective-permute-start.14 = (f32[96,8]{1,0:T(8,128)S(1)}, f32[96,8]{1,0:T(8,128)S(1)}, u32[]{:S(2)}, u32[]{:S(2)}) collective-permute-start(f32[96,8]{1,0:T(8,128)S(1)} %get-tuple-element.35), channel_id=1, source_target_pairs={{0,1},{1,2},{2,3},{3,4},{4,5},{5,6},{6,7},{7,0},{8,9},{9,10},{10,1... | collective-permute-start | bytes 9224 | tf_op jit(solution)/shard_map/ppermute | solution.py:19
  156.2 29.0 %collective-permute-start.15 = (f32[96,8]{1,0:T(8,128)S(1)}, f32[96,8]{1,0:T(8,128)S(1)}, u32[]{:S(2)}, u32[]{:S(2)}) collective-permute-start(f32[96,8]{1,0:T(8,128)S(1)} %get-tuple-element.36), channel_id=1, source_target_pairs={{1,0},{2,1},{3,2},{4,3},{5,4},{6,5},{7,6},{0,7},{9,8},{10,9},{11,1... | collective-permute-start | bytes 9224 | tf_op jit(solution)/shard_map/ppermute | solution.py:21
  160.4 24.9 %copy-start.9 = (pred[64]{0:T(512)(128)(4,1)S(1)}, pred[64]{0:T(512)(128)(4,1)}, u32[]{:S(2)}) copy-start(pred[64]{0:T(512)(128)(4,1)} %constant.82.clone.1) | copy-start | bytes 196
  160.4 25.1 %copy-start.8 = (pred[128]{0:T(512)(128)(4,1)S(1)}, pred[128]{0:T(512)(128)(4,1)}, u32[]{:S(2)}) copy-start(pred[128]{0:T(512)(128)(4,1)} %constant.83.clone.1) | copy-start | bytes 388
  (4 other events, 10.4 us)
where the time goes:
time: 188 us; the launch traced here: 187 us
  other arithmetic  88.8 us (47%)
  local copies, waits for them, and re-layouts  48.1 us (26%)
  starting transfers between devices  34.3 us (18%)
  waiting for transfers between devices  10.4 us (6%)
  matrix products  4.25 us (2%)
    add x1, other arithmetic, on_device(): thermal_anomaly + thermal_change_speed(initial_reflected_share, eastward_...  24.8 us
    add x1, other arithmetic, on_device(): thermal_anomaly + thermal_change_speed(repeated_reflected_share, eastward...  24.8 us
    add x1, other arithmetic, on_device(): thermal_anomaly + thermal_change_speed(thermal_anomaly, eastward_shift_ra...  22.8 us
    slice x8, local copies, waits for them, and re-layouts, with_halo(): lax.slice_in_dim(cells, cells.shape[dim] - width, cells.shape[dim], axis=...  16.2 us
    ppermute x8, starting transfers between devices, with_halo(): lax.ppermute(head, axis, [((i + 1) % count, i) for i in range(count)])  14.2 us
    scatter-add x1, other arithmetic, on_device(): jax.ops.segment_sum(absorbed, nearest_ground_index, num_segments=span_x *...  11.4 us
    all_to_all x2, starting transfers between devices, irradiance(): lax.all_to_all(sent, ('gx', 'gy'), split_axis=0, concat_axis=0, tiled=True)  10.1 us
    ppermute x8, starting transfers between devices, with_halo(): lax.ppermute(tail, axis, [(i, (i + 1) % count) for i in range(count)])  9.97 us
  transfers between devices with their start and end apart: 18, of which 5 were waited for; matrix products, arithmetic and copies ran while one was open for 72% of the time, Pallas kernels for 0%

commit v1 on v0

v1 whole, which is shorter than its diff:
```python
import functools

import jax
import jax.numpy as jnp
from jax import lax
from jax.experimental import pallas as pl
from jax.experimental.pallas import tpu as pltpu
from jax.sharding import PartitionSpec as P


MARGIN = 8
HEAT_GAIN = 0.02
SUB = 8
LANES = 128
EDGE = 4
PIECES = 4

VMEM = pl.BlockSpec(memory_space=pltpu.VMEM)
SMEM = pl.BlockSpec(memory_space=pltpu.SMEM)
HBM = pl.BlockSpec(memory_space=pltpu.HBM)


def swap_low(axis):
    return [(i, i ^ 1) for i in range(lax.axis_size(axis))]


def swap_high(axis):
    count = lax.axis_size(axis)
    return [(i, (i + 1 if i % 2 else i - 1) % count) for i in range(count)]


def is_even(axis):
    return lax.rem(lax.axis_index(axis), 2) == 0


def in_hbm(array):
    return pltpu.with_memory_space_constraint(array, pltpu.HBM)


def grant(mebibytes):
    return pltpu.CompilerParams(vmem_limit_bytes=mebibytes * 1024 * 1024)


def cost(flops, nbytes):
    return pl.CostEstimate(flops=flops, bytes_accessed=nbytes, transcendentals=0)


def lane_group():
    return lax.broadcasted_iota(jnp.int32, (SUB, LANES), 1) // EDGE


def pack_kernel(levels_per, q_hbm, n_hbm, qp_ref, np_ref, edge_a_ref, edge_b_ref, q_ref, n_ref, low_ref, high_ref, sems):
    levels, rows, _ = q_ref.shape
    tiles = rows // SUB
    groups = levels // levels_per
    group_of = lane_group()

    def copies(g):
        at = pl.ds(g * levels_per, levels_per)
        return (
            pltpu.make_async_copy(q_hbm.at[at], q_ref.at[at], sems.at[0, g]),
            pltpu.make_async_copy(n_hbm.at[at], n_ref.at[at], sems.at[1, g]),
        )

    @pl.loop(0, groups)
    def _(g):
        for copy in copies(g):
            copy.start()

    @pl.loop(0, groups)
    def _(g):
        for copy in copies(g):
            copy.wait()
        packed_q = jnp.zeros((SUB, LANES), jnp.float32)
        packed_n = jnp.zeros((SUB, LANES), jnp.float32)
        for t in range(tiles):
            for j in range(levels_per):
                k = t * levels_per + j
                level = g * levels_per + j
                mine = group_of == k
                q = q_ref[level, t * SUB : (t + 1) * SUB, :]
                n = n_ref[level, t * SUB : (t + 1) * SUB, :]
                turn = (EDGE * k + 2) % LANES
                packed_q = jnp.where(mine, pltpu.roll(q, turn, 1), packed_q)
                packed_n = jnp.where(mine, pltpu.roll(n, turn, 1), packed_n)
                at = pl.ds(pl.multiple_of(g * 2 * levels_per, 2 * levels_per) + 2 * j, 2)
                if t == 0:
                    low_ref[at, :] = q[0:2]
                if t == tiles - 1:
                    high_ref[at, :] = q[SUB - 2 : SUB]
        at = pl.ds(pl.multiple_of(g * SUB, SUB), SUB)
        qp_ref[at, :] = packed_q
        np_ref[at, :] = packed_n

    share_edges(edge_a_ref, edge_b_ref, low_ref, high_ref)


def share_edges(edge_a_ref, edge_b_ref, low_ref, high_ref):
    even = is_even("gx")
    edge_a_ref[...] = jnp.where(even, high_ref[...], low_ref[...])
    edge_b_ref[...] = jnp.where(even, low_ref[...], high_ref[...])


def levels_per_group(rows):
    return LANES // EDGE // (rows // SUB)


def pack(q, n):
    levels, rows, columns = q.shape
    per = levels_per_group(rows)
    packed = jax.ShapeDtypeStruct((levels // per * SUB, LANES), jnp.float32)
    edge = jax.ShapeDtypeStruct((levels * 2, columns), jnp.float32)
    return pl.pallas_call(
        functools.partial(pack_kernel, per),
        out_shape=(packed, packed, edge, edge),
        in_specs=[HBM, HBM],
        out_specs=(VMEM, VMEM, VMEM, VMEM),
        scratch_shapes=[
            pltpu.VMEM(q.shape, jnp.float32),
            pltpu.VMEM(q.shape, jnp.float32),
            pltpu.VMEM(edge.shape, jnp.float32),
            pltpu.VMEM(edge.shape, jnp.float32),
            pltpu.SemaphoreType.DMA((2, levels // per)),
        ],
        name="pack",
        compiler_params=grant(6),
        cost_estimate=cost(4_000_000, q.size * 8),
    )(in_hbm(q), in_hbm(n))


def stage_kernel(
    levels_per, coefficient, first_stage, last, base_hbm, q_hbm, e_hbm, n_hbm, u_hbm,
    edge_a_in, edge_b_in, own_ref, side_a_ref, side_b_ref, np_ref, out_hbm, *rest,
):
    if last:
        ground_ref, padded, base_ref, e_ref, n_ref, u_ref, out_ref, sems, done = rest
    else:
        packed_ref, edge_a_ref, edge_b_ref, padded, base_ref, e_ref, n_ref, u_ref, out_ref, low_ref, high_ref, sems, done = rest
    levels, rows, _ = out_ref.shape
    tiles = rows // SUB
    groups = levels // levels_per
    lane = lax.broadcasted_iota(jnp.int32, (SUB, LANES), 1)
    group_of = lane // EDGE
    member = lane % EDGE
    touched = jnp.logical_or(lane < 2, lane >= LANES - 2)
    even_x, even_y = is_even("gx"), is_even("gy")

    def field(g):
        at = pl.ds(g * levels_per, levels_per)
        return pltpu.make_async_copy(q_hbm.at[at], padded.at[at, pl.ds(SUB, rows)], sems.at[0, g])

    def others(g):
        at = pl.ds(g * levels_per, levels_per)
        found = [
            pltpu.make_async_copy(e_hbm.at[at], e_ref.at[at], sems.at[1, g]),
            pltpu.make_async_copy(n_hbm.at[at], n_ref.at[at], sems.at[2, g]),
            pltpu.make_async_copy(u_hbm.at[at], u_ref.at[at], sems.at[3, g]),
        ]
        if not first_stage:
            found.append(pltpu.make_async_copy(base_hbm.at[at], base_ref.at[at], sems.at[4, g]))
        return found

    def outgoing(g):
        at = pl.ds(g * levels_per, levels_per)
        return pltpu.make_async_copy(out_ref.at[at], out_hbm.at[at], done.at[g])

    @pl.loop(0, groups)
    def _(g):
        field(g).start()
        for copy in others(g):
            copy.start()

    field(0).wait()

    @pl.loop(0, groups)
    def _(g):
        @pl.when(g + 1 < groups)
        def _():
            field(g + 1).wait()

        for copy in others(g):
            copy.wait()
        for j in range(levels_per):
            level = g * levels_per + j
            rows_at = pl.ds(pl.multiple_of(g * 2 * levels_per, 2 * levels_per) + 2 * j, 2)
            got_a, got_b = edge_a_in[rows_at, :], edge_b_in[rows_at, :]
            padded[level, SUB - 2 : SUB, :] = jnp.where(even_x, got_b, got_a)
            padded[level, SUB + rows : SUB + rows + 2, :] = jnp.where(even_x, got_a, got_b)
        at = pl.ds(pl.multiple_of(g * SUB, SUB), SUB)
        side_a, side_b = side_a_ref[at, :], side_b_ref[at, :]
        right = jnp.where(even_y, side_a, side_b)
        left = jnp.where(even_y, side_b, side_a)
        own = own_ref[at, :]
        speed = np_ref[at, :]
        gap = jnp.where(
            member < 2,
            pltpu.roll(right - own, LANES - 2, 1),
            pltpu.roll(left - own, 2, 1),
        )
        before = pltpu.roll(gap, 1, 1)
        after = pltpu.roll(gap, LANES - 1, 1)
        rising = jnp.where(
            member == 0, 0.0, jnp.where(member == 1, 2.0 * before, jnp.where(member == 2, gap - 6.0 * after, gap))
        )
        falling = jnp.where(
            member == 0, gap, jnp.where(member == 1, gap - 6.0 * before, jnp.where(member == 2, 2.0 * after, 0.0))
        )
        mend = jnp.abs(speed) * jnp.where(speed >= 0.0, rising, falling)
        packed = jnp.zeros((SUB, LANES), jnp.float32)
        first = g * levels_per
        for t in range(tiles):
            here = slice(SUB + t * SUB, SUB + (t + 1) * SUB)
            tile = slice(t * SUB, (t + 1) * SUB)
            column = []
            for d in range(-2, levels_per + 2):
                level = first + d
                if d < 0:
                    level = jnp.maximum(level, 0)
                elif d >= levels_per:
                    level = jnp.minimum(level, levels - 1)
                column.append(padded[level, here, :])
            for j in range(levels_per):
                k = t * levels_per + j
                level = first + j
                q = column[j + 2]
                triple = 3.0 * q

                def moved(back_two, back, ahead, ahead_two, velocity):
                    positive = velocity >= 0.0
                    near = jnp.where(positive, back, ahead)
                    far = jnp.where(positive, back_two, ahead_two)
                    return jnp.abs(velocity) * (
                        (far - 8.0 * near) + (2.0 * (back + ahead) + triple)
                    )

                def row(offset):
                    return padded[level, SUB + t * SUB + offset : SUB + (t + 1) * SUB + offset, :]

                total = moved(row(-2), row(-1), row(1), row(2), e_ref[level, tile, :])
                total += moved(column[j], column[j + 1], column[j + 3], column[j + 4], u_ref[level, tile, :])
                total += moved(
                    pltpu.roll(q, 2, 1),
                    pltpu.roll(q, 1, 1),
                    pltpu.roll(q, LANES - 1, 1),
                    pltpu.roll(q, LANES - 2, 1),
                    n_ref[level, tile, :],
                )
                total += jnp.where(touched, pltpu.roll(mend, (2 * LANES - 2 - EDGE * k) % LANES, 1), 0.0)
                base = q if first_stage else base_ref[level, tile, :]
                result = base - (coefficient / 6.0) * total
                out_ref[level, tile, :] = result
                if last:
                    continue
                packed = jnp.where(group_of == k, pltpu.roll(result, (EDGE * k + 2) % LANES, 1), packed)
                edge_at = pl.ds(pl.multiple_of(g * 2 * levels_per, 2 * levels_per) + 2 * j, 2)
                if t == 0:
                    low_ref[edge_at, :] = result[0:2]
                if t == tiles - 1:
                    high_ref[edge_at, :] = result[SUB - 2 : SUB]
        if not last:
            packed_ref[at, :] = packed
        outgoing(g).start()

    if last:
        ground_ref[...] = out_ref[0]
    else:
        share_edges(edge_a_ref, edge_b_ref, low_ref, high_ref)

    @pl.loop(0, groups)
    def _(g):
        outgoing(g).wait()


def stage(base, q, winds, edges, packed_winds, coefficient, first_stage=False, last=False):
    levels, rows, columns = q.shape
    per = levels_per_group(rows)
    whole = pltpu.HBM(q.shape, jnp.float32)
    packed = jax.ShapeDtypeStruct((levels // per * SUB, LANES), jnp.float32)
    edge = jax.ShapeDtypeStruct((levels * 2, columns), jnp.float32)
    ground = jax.ShapeDtypeStruct((rows, columns), jnp.float32)
    outs = (whole, ground) if last else (whole, packed, edge, edge)
    return pl.pallas_call(
        functools.partial(stage_kernel, per, coefficient, first_stage, last),
        out_shape=outs,
        in_specs=[HBM] * 5 + [VMEM] * 6,
        out_specs=(HBM,) + (VMEM,) * (len(outs) - 1),
        scratch_shapes=[
            pltpu.VMEM((levels, rows + 2 * SUB, columns), jnp.float32),
            pltpu.VMEM((SUB, LANES) if first_stage else q.shape, jnp.float32),
            *(pltpu.VMEM(q.shape, jnp.float32) for _ in range(4)),
            *(pltpu.VMEM(edge.shape, jnp.float32) for _ in range(0 if last else 2)),
            pltpu.SemaphoreType.DMA((5, levels // per)),
            pltpu.SemaphoreType.DMA((levels // per,)),
        ],
        name="stage",
        compiler_params=grant(16),
        cost_estimate=cost(24_000_000, q.size * 24),
    )(*map(in_hbm, (base, q, *winds)), *edges, packed_winds)


def swap(array, axis):
    a = lax.ppermute(array[0], axis, swap_low(axis))
    b = lax.ppermute(array[1], axis, swap_high(axis))
    return a, b


def neighbours(packed, edge_a, edge_b):
    sides = swap((packed, packed), "gy")
    edges = swap((edge_a, edge_b), "gx")
    return *edges, packed, *sides


def exchange(sent):
    return lax.all_to_all(sent, ("gx", "gy"), split_axis=0, concat_axis=0, tiled=True)


def project(light, blocks_ref, source_ref, live_ref, sent_hbm, sent_ref, done, ready=None):
    peers, slots, width, _ = blocks_ref.shape
    bands = light.shape[1]
    nothing = jnp.zeros((bands, width), jnp.bfloat16)
    pieces = done.shape[0]
    share = peers // pieces

    def outgoing(p):
        at = pl.ds(p * share, share)
        return pltpu.make_async_copy(sent_ref.at[at], sent_hbm.at[at], done.at[p])

    for p in range(pieces):
        if ready is not None:
            ready(p)

        @pl.loop(p * share, (p + 1) * share, unroll=4)
        def _(r):
            for c in range(0, slots, 2):
                one = light[source_ref[c, r]]
                two = light[source_ref[c + 1, r]]
                left = jnp.concatenate(
                    [jnp.concatenate([one, nothing], axis=1), jnp.concatenate([nothing, two], axis=1)], axis=0
                )
                right = blocks_ref[r, c : c + 2].reshape(2 * width, width)
                got = jnp.dot(left, right, preferred_element_type=jnp.float32)
                for d in range(2):
                    scale = jnp.where(c + d < live_ref[0, r], 0.5 / width, 0.0)
                    sent_ref[r, c + d] = got[d * bands : (d + 1) * bands] * scale

        outgoing(p).start()
    for p in range(pieces):
        outgoing(p).wait()


def first_kernel(emitted_ref, blocks_ref, source_ref, live_ref, sent_hbm, light, sent_ref, done):
    blocks, _, width = light.shape
    for f in range(blocks):
        light[f] = emitted_ref[:, f * width : (f + 1) * width].astype(jnp.bfloat16)
    project(light, blocks_ref, source_ref, live_ref, sent_hbm, sent_ref, done)


def gather_light(arrived_ref, target_ref, total):
    peers, slots = arrived_ref.shape[:2]
    total[...] = jnp.zeros_like(total)

    @pl.loop(0, peers, unroll=4)
    def _(s):
        for c in range(slots):
            g = target_ref[c, s]
            total[g] = total[g] + arrived_ref[s, c]


def second_kernel(
    arrived_ref, target_ref, emitted_ref, albedo_ref, blocks_hbm, source_ref, live_ref, sent_hbm,
    light, total, blocks_ref, sent_ref, done, loaded,
):
    pieces = loaded.shape[0]
    share = blocks_ref.shape[0] // pieces

    def incoming(p):
        at = pl.ds(p * share, share)
        return pltpu.make_async_copy(blocks_hbm.at[at], blocks_ref.at[at], loaded.at[p])

    for p in range(pieces):
        incoming(p).start()
    gather_light(arrived_ref, target_ref, total)
    blocks, _, width = light.shape
    for f in range(blocks):
        at = slice(f * width, (f + 1) * width)
        light[f] = (emitted_ref[:, at] + albedo_ref[:, at] * total[f]).astype(jnp.bfloat16)
    project(light, blocks_ref, source_ref, live_ref, sent_hbm, sent_ref, done, lambda p: incoming(p).wait())


def last_kernel(
    rows, columns, arrived_ref, target_ref, emitted_ref, albedo_ref, ground_ref,
    leaving_ref, inner_ref, rim_a_ref, rim_b_ref, total, heat, cells,
):
    gather_light(arrived_ref, target_ref, total)
    blocks, _, width = total.shape
    span_x, span_y = rows + 2 * MARGIN, columns + 2 * MARGIN
    x_index = lax.broadcasted_iota(jnp.int32, (span_x, width), 0).astype(jnp.float32)
    y_index = lax.broadcasted_iota(jnp.int32, (2 * columns, width), 0).astype(jnp.float32)
    for f in range(blocks):
        at = slice(f * width, (f + 1) * width)
        light = total[f]
        albedo = albedo_ref[:, at]
        leaving_ref[:, at] = emitted_ref[:, at] + albedo * light
        absorbed = HEAT_GAIN * jnp.sum((1.0 - albedo) * light, axis=0, keepdims=True)
        place = ground_ref[f : f + 1, :].astype(jnp.float32)
        x = jnp.floor((place + 0.5) * (1.0 / span_y))
        y = place - span_y * x
        x = jnp.where(x < MARGIN, x + (span_x - MARGIN), x - MARGIN)
        y = jnp.where(y < MARGIN, y + (2 * columns - MARGIN), y - MARGIN)
        coarse = absorbed.astype(jnp.bfloat16).astype(jnp.float32)
        fine = absorbed - coarse
        hit = x_index == x
        heat[0:span_x, at] = jnp.where(hit, coarse, 0.0).astype(jnp.bfloat16)
        heat[span_x : 2 * span_x, at] = jnp.where(hit, fine, 0.0).astype(jnp.bfloat16)
        cells[:, at] = jnp.where(y_index == y, 1.0, 0.0).astype(jnp.bfloat16)
    both = lax.dot_general(
        heat[...], cells[...], (((1,), (1,)), ((), ())), preferred_element_type=jnp.float32
    )
    field = both[0:span_x] + both[span_x : 2 * span_x]
    inner_ref[...] = field[0:rows]
    upper = field[rows : rows + MARGIN]
    lower = field[rows + MARGIN : rows + 2 * MARGIN]
    even = is_even("gx")
    rim_a_ref[...] = jnp.where(even, upper, lower)
    rim_b_ref[...] = jnp.where(even, lower, upper)


def fold_kernel(inner_ref, rim_a_ref, rim_b_ref, middle_ref, side_ref):
    rows, columns = middle_ref.shape
    even = is_even("gx")
    for half, ref in ((0, middle_ref), (1, side_ref)):
        at = slice(half * columns, (half + 1) * columns)
        rim_a, rim_b = rim_a_ref[:, at], rim_b_ref[:, at]
        ref[...] = inner_ref[:, at]
        ref[0:MARGIN, :] = ref[0:MARGIN, :] + jnp.where(even, rim_b, rim_a)
        ref[rows - MARGIN : rows, :] = ref[rows - MARGIN : rows, :] + jnp.where(even, rim_a, rim_b)


def finish_kernel(field_ref, ground_ref, middle_ref, side_a_ref, side_b_ref, out_ref, level, sem):
    lane = lax.broadcasted_iota(jnp.int32, level.shape, 1)
    columns = level.shape[1]
    even = is_even("gy")
    left = jnp.where(even, side_b_ref[...], side_a_ref[...])
    right = jnp.where(even, side_a_ref[...], side_b_ref[...])
    level[...] = (
        ground_ref[...]
        + middle_ref[...]
        + jnp.where(lane < MARGIN, left, 0.0)
        + jnp.where(lane >= columns - MARGIN, right, 0.0)
    )
    copy = pltpu.make_async_copy(level, out_ref.at[0], sem)
    copy.start()
    copy.wait()


def step(
    thermal_anomaly,
    eastward_shift_ratio,
    northward_shift_ratio,
    upward_shift_ratio,
    emitted_power,
    albedo_values,
    visibility_matrices,
    active_pairing_totals,
    sender_panel_group,
    receiver_panel_group,
    nearest_ground_index,
):
    _, rows, columns = thermal_anomaly.shape
    bands, faces = emitted_power.shape
    blocks = visibility_matrices[0]
    peers, slots, width, _ = blocks.shape
    owned = faces // width
    source = jnp.transpose(sender_panel_group[0])
    target = jnp.transpose(receiver_panel_group[:, 0, :])
    message = pltpu.HBM((peers, slots, bands, width), jnp.float32)
    light = pltpu.VMEM((owned, bands, width), jnp.bfloat16)
    total = pltpu.VMEM((owned, bands, width), jnp.float32)
    winds = (eastward_shift_ratio, northward_shift_ratio, upward_shift_ratio)

    sent = pl.pallas_call(
        first_kernel,
        out_shape=message,
        in_specs=[VMEM, VMEM, SMEM, SMEM],
        out_specs=HBM,
        scratch_shapes=[light, pltpu.VMEM(message.shape, jnp.float32), pltpu.SemaphoreType.DMA((PIECES,))],
        name="first",
        compiler_params=grant(4),
        cost_estimate=cost(10_000_000, blocks.size * 2),
    )(emitted_power, blocks, source, active_pairing_totals)
    packed, packed_winds, *rows_sent = pack(thermal_anomaly, northward_shift_ratio)
    edges = neighbours(packed, *rows_sent)
    arrived = exchange(sent)

    one, *sides = stage(thermal_anomaly, thermal_anomaly, winds, edges, packed_winds, 1.0 / 3.0, first_stage=True)
    edges = neighbours(*sides)

    sent = pl.pallas_call(
        second_kernel,
        out_shape=message,
        in_specs=[VMEM, SMEM, VMEM, VMEM, HBM, SMEM, SMEM],
        out_specs=HBM,
        scratch_shapes=[
            light,
            total,
            pltpu.VMEM(blocks.shape, jnp.bfloat16),
            pltpu.VMEM(message.shape, jnp.float32),
            pltpu.SemaphoreType.DMA((PIECES,)),
            pltpu.SemaphoreType.DMA((PIECES,)),
        ],
        name="second",
        compiler_params=grant(6 + 6 * peers // 32),
        cost_estimate=cost(12_000_000, blocks.size * 2),
    )(arrived, target, emitted_power, albedo_values, in_hbm(blocks), source, active_pairing_totals)
    arrived = exchange(sent)

    two, *sides = stage(thermal_anomaly, one, winds, edges, packed_winds, 1.0 / 2.0)
    edges = neighbours(*sides)

    span_x = rows + 2 * MARGIN
    rim = jax.ShapeDtypeStruct((MARGIN, 2 * columns), jnp.float32)
    leaving, inner, *rims = pl.pallas_call(
        functools.partial(last_kernel, rows, columns),
        out_shape=(
            jax.ShapeDtypeStruct((bands, faces), jnp.float32),
            jax.ShapeDtypeStruct((rows, 2 * columns), jnp.float32),
            rim,
            rim,
        ),
        in_specs=[VMEM, SMEM, VMEM, VMEM, VMEM],
        out_specs=(VMEM,) * 4,
        scratch_shapes=[
            total,
            pltpu.VMEM((2 * span_x, faces), jnp.bfloat16),
            pltpu.VMEM((2 * columns, faces), jnp.bfloat16),
        ],
        name="last",
        compiler_params=grant(8),
        cost_estimate=cost(16_000_000, arrived.size * 4),
    )(arrived, target, emitted_power, albedo_values, nearest_ground_index.reshape(owned, width))
    rims = swap(rims, "gx")

    three, ground = stage(thermal_anomaly, two, winds, edges, packed_winds, 1.0, last=True)

    flat = jax.ShapeDtypeStruct((rows, columns), jnp.float32)
    middle, side = pl.pallas_call(
        fold_kernel,
        out_shape=(flat, flat),
        in_specs=[VMEM] * 3,
        out_specs=(VMEM, VMEM),
        name="fold",
        compiler_params=grant(2),
        cost_estimate=cost(500_000, flat.size * 8),
    )(inner, *rims)
    sides = swap((side, side), "gy")

    renewed = pl.pallas_call(
        finish_kernel,
        out_shape=jax.ShapeDtypeStruct(thermal_anomaly.shape, jnp.float32),
        in_specs=[HBM, VMEM, VMEM, VMEM, VMEM],
        out_specs=HBM,
        scratch_shapes=[pltpu.VMEM((rows, columns), jnp.float32), pltpu.SemaphoreType.DMA],
        input_output_aliases={0: 0},
        name="finish",
        compiler_params=grant(2),
        cost_estimate=cost(500_000, flat.size * 8),
    )(three, ground, middle, *sides)
    return renewed, leaving


def solution(mesh):
    in_specs = (
        P(None, "gx", "gy"),
        P(None, "gx", "gy"),
        P(None, "gx", "gy"),
        P(None, "gx", "gy"),
        P(None, ("gx", "gy")),
        P(None, ("gx", "gy")),
        P(("gx", "gy"), None, None, None, None),
        P(("gx", "gy"), None),
        P(("gx", "gy"), None, None),
        P(None, ("gx", "gy"), None),
        P(("gx", "gy")),
    )
    out_specs = (P(None, "gx", "gy"), P(None, ("gx", "gy")))
    return jax.shard_map(step, mesh=mesh, in_specs=in_specs, out_specs=out_specs, check_vma=False)
```

time: 188 us -> 100 us (0.53)
  other arithmetic: 88.8 us -> 0 us
  local copies, waits for them, and re-layouts: 48.1 us -> 3.85 us
  Pallas kernels: 0 us -> 38.1 us
  blocking collectives: 0 us -> 22.8 us
  starting transfers between devices: 34.3 us -> 22.9 us
  matrix products: 4.25 us -> 0 us
    add x5 -> x0, other arithmetic: 73.1 us -> none  [the longest x1 24.8 us: on_device(): thermal_anomaly + thermal_change_speed(initial_reflected_share, eastward_...]
    pallas_call x0 -> x9, Pallas kernels: none -> 38.1 us  [the longest x3 25.5 us: stage(): pl.pallas_call(functools.partial(stage_kernel, per, coefficient, first_st...]
    slice x20 -> x0, local copies, waits for them, and re-layouts: 27.4 us -> none  [the longest x8 16.2 us: with_halo(): lax.slice_in_dim(cells, cells.shape[dim] - width, cells.shape[dim], axis=...]
    all_to_all x0 -> x1, blocking collectives: none -> 22.8 us  [exchange(): lax.all_to_all(sent, ('gx', 'gy'), split_axis=0, concat_axis=0, tiled=True)]
    ppermute x6 -> x0, local copies, waits for them, and re-layouts: 13.6 us -> none  [the longest x3 6.84 us: with_halo(): lax.ppermute(tail, axis, [(i, (i + 1) % count) for i in range(count)])]
    scatter-add x2 -> x0, other arithmetic: 11.5 us -> none  [the longest x1 11.4 us: on_device(): jax.ops.segment_sum(absorbed, nearest_ground_index, num_segments=span_x *...]
    all_to_all x2 -> x1, starting transfers between devices: 10.1 us -> 2.98 us  [exchange(): lax.all_to_all(sent, ('gx', 'gy'), split_axis=0, concat_axis=0, tiled=True)]
    ppermute x16, starting transfers between devices: 24.2 us -> 19.9 us  [the longest x8 11.5 us: swap(): b = lax.ppermute(array[1], axis, swap_high(axis))]
  transfers between devices with their start and end apart: 18 -> 17, of which waited for: 5 -> 5; matrix products, arithmetic and copies ran while one was open for 72% -> 0% of each run, Pallas kernels for 0% -> 31%
where the time goes in v1:
time: 100 us; the launch traced here: 99.2 us
  Pallas kernels  38.1 us (38%)
  starting transfers between devices  22.9 us (23%)
  blocking collectives  22.8 us (23%)
  waiting for transfers between devices  10.8 us (11%)
  local copies, waits for them, and re-layouts  3.85 us (4%)
    pallas_call x3, Pallas kernels, stage(): pl.pallas_call(functools.partial(stage_kernel, per, coefficient, first_st...  25.5 us
    all_to_all x1, blocking collectives, exchange(): lax.all_to_all(sent, ('gx', 'gy'), split_axis=0, concat_axis=0, tiled=True)  22.8 us
    ppermute x8, starting transfers between devices, swap(): b = lax.ppermute(array[1], axis, swap_high(axis))  11.5 us
    ppermute x8, waiting for transfers between devices, swap(): b = lax.ppermute(array[1], axis, swap_high(axis))  9.92 us
    ppermute x8, starting transfers between devices, swap(): a = lax.ppermute(array[0], axis, swap_low(axis))  8.47 us
    unnamed x18, local copies, waits for them, and re-layouts  3.85 us
    pallas_call x1, Pallas kernels, step(): pl.pallas_call(second_kernel, out_shape=message, in_specs=[VMEM, SMEM, VM...  3.71 us
    pallas_call x1, Pallas kernels, pack(): pl.pallas_call(functools.partial(pack_kernel, per), out_shape=(packed, pa...  3.48 us
  transfers between devices with their start and end apart: 17, of which 5 were waited for; matrix products, arithmetic and copies ran while one was open for 0% of the time, Pallas kernels for 31%

profile of v1, /device:TPU:1, one launch (start us, length us, event | category | flops | bytes accessed | tf_op | source)
XLA Modules:
  0.0 99.2 jit_solution(2058805001162565977)
XLA Ops:
  0.7 1.6 %copy-done = bf16[1,32,2,128,128]{4,3,2,1,0:T(8,128)(2,1)S(1)} copy-done((bf16[1,32,2,128,128]{4,3,2,1,0:T(8,128)(2,1)S(1)}, bf16[1,32,2,128,128]{4,3,2,1,0:T(8,128)(2,1)}, u32[]{:S(2)}) %copy-start) | copy-done | bytes 2097176
  2.3 0.9 copy-done.1
  4.5 2.6 %first.1 = f32[32,2,16,128]{3,2,1,0:T(8,128)} custom-call(f32[16,2048]{1,0:T(8,128)S(1)} %copy-done.1, bf16[32,2,128,128]{3,2,1,0:T(8,128)(2,1)S(1)} %bitcast.9, s32[2,32]{1,0:T(2,128)S(1)} %bitcast.11, s32[1,32]{1,0:T(1,128)S(1)} %copy-done.8), custom_call_target="tpu_custom_call" | custom-call | flops 10000000 | bytes 2097152 | tf_op jit(solution)/shard_map/first/pallas_call | solution.py:481
  7.1 22.8 %all_to_all.10.arrived_ref = f32[32,2,16,128]{3,2,1,0:T(8,128)S(1)} all-to-all(f32[32,2,16,128]{3,2,1,0:T(8,128)} %first.1), channel_id=1, replica_groups=mesh['gx'=4,'gy'=8] {'gx','gy'}, dimensions={0} | all-to-all | bytes 1048576 | tf_op jit(solution)/shard_map/all_to_all | solution.py:314
  30.0 3.7 %second.1 = f32[32,2,16,128]{3,2,1,0:T(8,128)} custom-call(f32[32,2,16,128]{3,2,1,0:T(8,128)S(1)} %all_to_all.10.arrived_ref, s32[2,32]{1,0:T(2,128)S(1)} %bitcast.13, f32[16,2048]{1,0:T(8,128)S(1)} %copy-done.2, f32[16,2048]{1,0:T(8,128)S(1)} %copy-done.3, bf16[32,2,128,128]{3,2,1,0:T(8,128)(2,1)} %bitcast.8, s32[2,32]{1,0:T(2,128)S(1)} %bitcast.12, ...), custom_call_target="tpu_custom_call" | custom-call | flops 12000000 | bytes 2097152 | tf_op jit(solution)/shard_map/second/pallas_call | solution.py:498
  33.7 3.0 %all-to-all-start.1 = ((f32[32,2,16,128]{3,2,1,0:T(8,128)}), f32[32,2,16,128]{3,2,1,0:T(8,128)S(1)}, u32[]{:S(2)}, u32[]{:S(2)}) async-start(f32[32,2,16,128]{3,2,1,0:T(8,128)} %second.1), calls=%async_computation.1 | async-start | bytes 1048576 | tf_op jit(solution)/shard_map/all_to_all | solution.py:314
  36.7 3.5 %pack.1 = (f32[128,128]{1,0:T(8,128)S(1)}, f32[128,128]{1,0:T(8,128)S(1)}, f32[128,128]{1,0:T(8,128)S(1)}, f32[128,128]{1,0:T(8,128)S(1)}) custom-call(f32[64,64,128]{2,1,0:T(8,128)} %base_hbm.5, f32[64,64,128]{2,1,0:T(8,128)} %n_hbm.7), custom_call_target="tpu_custom_call" | custom-call | flops 4000000 | bytes 4194304 | tf_op jit(solution)/shard_map/pack/pallas_call | solution.py:113
  40.2 1.4 %collective-permute-start.2 = (f32[128,128]{1,0:T(8,128)S(1)}, f32[128,128]{1,0:T(8,128)S(1)}, u32[]{:S(2)}, u32[]{:S(2)}) collective-permute-start(f32[128,128]{1,0:T(8,128)S(1)} %get-tuple-element.24.own_ref), channel_id=1, source_target_pairs={{0,1},{1,0},{2,3},{3,2},{4,5},{5,4},{6,7},{7,6},{8,9},{9,8},{10,11... | collective-permute-start | bytes 196616 | tf_op jit(solution)/shard_map/ppermute | solution.py:302
  41.6 3.2 %collective-permute-start.3 = (f32[128,128]{1,0:T(8,128)S(1)}, f32[128,128]{1,0:T(8,128)S(1)}, u32[]{:S(2)}, u32[]{:S(2)}) collective-permute-start(f32[128,128]{1,0:T(8,128)S(1)} %get-tuple-element.24.own_ref), channel_id=1, source_target_pairs={{0,7},{1,2},{2,1},{3,4},{4,3},{5,6},{6,5},{7,0},{8,15},{9,10},{10,... | collective-permute-start | bytes 196616 | tf_op jit(solution)/shard_map/ppermute | solution.py:303
  44.8 0.9 collective-permute-start
  45.7 1.1 %collective-permute-start.1 = (f32[128,128]{1,0:T(8,128)S(1)}, f32[128,128]{1,0:T(8,128)S(1)}, u32[]{:S(2)}, u32[]{:S(2)}) collective-permute-start(f32[128,128]{1,0:T(8,128)S(1)} %get-tuple-element.23), channel_id=1, source_target_pairs={{0,24},{8,16},{16,8},{24,0},{1,25},{9,17},{17,9},{25,1},{2,26},{10... | collective-permute-start | bytes 196616 | tf_op jit(solution)/shard_map/ppermute | solution.py:303
  46.8 4.7 %collective-permute-done.3.side_b_ref = f32[128,128]{1,0:T(8,128)S(1)} collective-permute-done((f32[128,128]{1,0:T(8,128)S(1)}, f32[128,128]{1,0:T(8,128)S(1)}, u32[]{:S(2)}, u32[]{:S(2)}) %collective-permute-start.3) | collective-permute-done | bytes 65568 | tf_op jit(solution)/shard_map/ppermute | solution.py:303
  51.6 9.2 %stage.3 = (f32[64,64,128]{2,1,0:T(8,128)}, f32[128,128]{1,0:T(8,128)S(1)}, f32[128,128]{1,0:T(8,128)S(1)}, f32[128,128]{1,0:T(8,128)S(1)}) custom-call(f32[64,64,128]{2,1,0:T(8,128)} %base_hbm.5, f32[64,64,128]{2,1,0:T(8,128)} %base_hbm.5, f32[64,64,128]{2,1,0:T(8,128)} %e_hbm.5, f32[64,64,128]{2,1,0:T(8,128)} %n_hbm.7, f32[64,64,128]{2,1,0:T(8,128)} %u_hbm.5, ...), custom_call_target="tpu_custom_call" | custom-call | flops 24000000 | bytes 12582912 | tf_op jit(solution)/shard_map/stage/pallas_call | solution.py:282
  61.1 2.0 %collective-permute-start.4 = (f32[128,128]{1,0:T(8,128)S(1)}, f32[128,128]{1,0:T(8,128)S(1)}, u32[]{:S(2)}, u32[]{:S(2)}) collective-permute-start(f32[128,128]{1,0:T(8,128)S(1)} %get-tuple-element.27), channel_id=1, source_target_pairs={{0,8},{8,0},{16,24},{24,16},{1,9},{9,1},{17,25},{25,17},{2,10},{10... | collective-permute-start | bytes 196616 | tf_op jit(solution)/shard_map/ppermute | solution.py:302
  63.1 1.1 %collective-permute-start.5 = (f32[128,128]{1,0:T(8,128)S(1)}, f32[128,128]{1,0:T(8,128)S(1)}, u32[]{:S(2)}, u32[]{:S(2)}) collective-permute-start(f32[128,128]{1,0:T(8,128)S(1)} %get-tuple-element.28), channel_id=1, source_target_pairs={{0,24},{8,16},{16,8},{24,0},{1,25},{9,17},{17,9},{25,1},{2,26},{10... | collective-permute-start | bytes 196616 | tf_op jit(solution)/shard_map/ppermute | solution.py:303
  64.2 2.5 %collective-permute-done.7.side_b_ref = f32[128,128]{1,0:T(8,128)S(1)} collective-permute-done((f32[128,128]{1,0:T(8,128)S(1)}, f32[128,128]{1,0:T(8,128)S(1)}, u32[]{:S(2)}, u32[]{:S(2)}) %collective-permute-start.7) | collective-permute-done | bytes 65568 | tf_op jit(solution)/shard_map/ppermute | solution.py:303
  66.8 8.9 %stage.4 = (f32[64,64,128]{2,1,0:T(8,128)}, f32[128,128]{1,0:T(8,128)S(1)}, f32[128,128]{1,0:T(8,128)S(1)}, f32[128,128]{1,0:T(8,128)S(1)}) custom-call(f32[64,64,128]{2,1,0:T(8,128)} %base_hbm.5, f32[64,64,128]{2,1,0:T(8,128)} %get-tuple-element.26.q_hbm, f32[64,64,128]{2,1,0:T(8,128)} %e_hbm.5, f32[64,64,128]{2,1,0:T(8,128)} %n_hbm.7, ...), custom_call_target="tpu_custom_call" | custom-call | flops 24000000 | bytes 12582912 | tf_op jit(solution)/shard_map/stage/pallas_call | solution.py:282
  75.7 2.9 %collective-permute-start.10 = (f32[128,128]{1,0:T(8,128)S(1)}, f32[128,128]{1,0:T(8,128)S(1)}, u32[]{:S(2)}, u32[]{:S(2)}) collective-permute-start(f32[128,128]{1,0:T(8,128)S(1)} %get-tuple-element.33.own_ref), channel_id=1, source_target_pairs={{0,1},{1,0},{2,3},{3,2},{4,5},{5,4},{6,7},{7,6},{8,9},{9,8},{10,11... | collective-permute-start | bytes 196616 | tf_op jit(solution)/shard_map/ppermute | solution.py:302
  78.6 2.0 %collective-permute-start.11 = (f32[128,128]{1,0:T(8,128)S(1)}, f32[128,128]{1,0:T(8,128)S(1)}, u32[]{:S(2)}, u32[]{:S(2)}) collective-permute-start(f32[128,128]{1,0:T(8,128)S(1)} %get-tuple-element.33.own_ref), channel_id=1, source_target_pairs={{0,7},{1,2},{2,1},{3,4},{4,3},{5,6},{6,5},{7,0},{8,15},{9,10},{10,... | collective-permute-start | bytes 196616 | tf_op jit(solution)/shard_map/ppermute | solution.py:303
  81.2 1.1 %collective-permute-start.9 = (f32[128,128]{1,0:T(8,128)S(1)}, f32[128,128]{1,0:T(8,128)S(1)}, u32[]{:S(2)}, u32[]{:S(2)}) collective-permute-start(f32[128,128]{1,0:T(8,128)S(1)} %get-tuple-element.32), channel_id=1, source_target_pairs={{0,24},{8,16},{16,8},{24,0},{1,25},{9,17},{17,9},{25,1},{2,26},{10... | collective-permute-start | bytes 196616 | tf_op jit(solution)/shard_map/ppermute | solution.py:303
  82.3 2.1 %last.1 = (f32[16,2048]{1,0:T(8,128)}, f32[64,256]{1,0:T(8,128)S(1)}, f32[8,256]{1,0:T(8,128)S(1)}, f32[8,256]{1,0:T(8,128)S(1)}) custom-call(f32[32,2,16,128]{3,2,1,0:T(8,128)S(1)} %all-to-all-done.1.arrived_ref, s32[2,32]{1,0:T(2,128)S(1)} %bitcast.14, f32[16,2048]{1,0:T(8,128)S(1)} %copy-done.2, f32[16,2048]{1,0:T(8,128)S(1)} %copy-done.3, ...), custom_call_target="tpu_custom_call" | custom-call | flops 16000000 | bytes 524288 | tf_op jit(solution)/shard_map/last/pallas_call | solution.py:522
  86.1 2.6 %collective-permute-done.13.rim_b_ref = f32[8,256]{1,0:T(8,128)S(1)} collective-permute-done((f32[8,256]{1,0:T(8,128)S(1)}, f32[8,256]{1,0:T(8,128)S(1)}, u32[]{:S(2)}, u32[]{:S(2)}) %collective-permute-start.13) | collective-permute-done | bytes 8224 | tf_op jit(solution)/shard_map/ppermute | solution.py:303
  88.8 2.3 %collective-permute-start.15 = (f32[64,128]{1,0:T(8,128)S(1)}, f32[64,128]{1,0:T(8,128)S(1)}, u32[]{:S(2)}, u32[]{:S(2)}) collective-permute-start(f32[64,128]{1,0:T(8,128)S(1)} %get-tuple-element.40), channel_id=1, source_target_pairs={{0,7},{1,2},{2,1},{3,4},{4,3},{5,6},{6,5},{7,0},{8,15},{9,10},{10,... | collective-permute-start | bytes 98312 | tf_op jit(solution)/shard_map/ppermute | solution.py:303
  91.1 7.4 %stage.5 = (f32[64,64,128]{2,1,0:T(8,128)}, f32[64,128]{1,0:T(8,128)S(1)}) custom-call(f32[64,64,128]{2,1,0:T(8,128)} %base_hbm.5, f32[64,64,128]{2,1,0:T(8,128)} %get-tuple-element.30.q_hbm, f32[64,64,128]{2,1,0:T(8,128)} %e_hbm.5, f32[64,64,128]{2,1,0:T(8,128)} %n_hbm.7, f32[64,64,128]{2,1,0:T(8,128)} %u_hbm.5, ...), custom_call_target="tpu_custom_call" | custom-call | flops 24000000 | bytes 12582912 | tf_op jit(solution)/shard_map/stage/pallas_call | solution.py:282
  (38 shorter events, 4.9 us)
Async XLA Ops:
  0.6 29.3 %copy-start.6 = (s32[1,32,2]{1,2,0:T(2,128)S(1)}, s32[1,32,2]{1,2,0:T(2,128)}, u32[]{:S(2)}) copy-start(s32[1,32,2]{1,2,0:T(2,128)} %param.19) | copy-start | bytes 772
  0.6 29.3 %copy-start.7 = (s32[32,1,2]{0,2,1:T(2,128)S(1)}, s32[32,1,2]{0,2,1:T(2,128)}, u32[]{:S(2)}) copy-start(s32[32,1,2]{0,2,1:T(2,128)} %param.20) | copy-start | bytes 772
  0.7 1.6 %copy-start = (bf16[1,32,2,128,128]{4,3,2,1,0:T(8,128)(2,1)S(1)}, bf16[1,32,2,128,128]{4,3,2,1,0:T(8,128)(2,1)}, u32[]{:S(2)}) copy-start(bf16[1,32,2,128,128]{4,3,2,1,0:T(8,128)(2,1)} %param.17) | copy-start | bytes 6291460
  2.3 0.9 copy-start.1
  4.5 25.5 %copy-start.2 = (f32[16,2048]{1,0:T(8,128)S(1)}, f32[16,2048]{1,0:T(8,128)}, u32[]{:S(2)}) copy-start(f32[16,2048]{1,0:T(8,128)} %emitted_ref.5) | copy-start | bytes 393220
  4.5 25.5 %copy-start.3 = (f32[16,2048]{1,0:T(8,128)S(1)}, f32[16,2048]{1,0:T(8,128)}, u32[]{:S(2)}) copy-start(f32[16,2048]{1,0:T(8,128)} %albedo_ref.3) | copy-start | bytes 393220
  33.7 48.6 %all-to-all-start.1 = ((f32[32,2,16,128]{3,2,1,0:T(8,128)}), f32[32,2,16,128]{3,2,1,0:T(8,128)S(1)}, u32[]{:S(2)}, u32[]{:S(2)}) async-start(f32[32,2,16,128]{3,2,1,0:T(8,128)} %second.1), calls=%async_computation.1 | async-start | bytes 1048576 | tf_op jit(solution)/shard_map/all_to_all | solution.py:314
  40.2 6.7 %collective-permute-start.2 = (f32[128,128]{1,0:T(8,128)S(1)}, f32[128,128]{1,0:T(8,128)S(1)}, u32[]{:S(2)}, u32[]{:S(2)}) collective-permute-start(f32[128,128]{1,0:T(8,128)S(1)} %get-tuple-element.24.own_ref), channel_id=1, source_target_pairs={{0,1},{1,0},{2,3},{3,2},{4,5},{5,4},{6,7},{7,6},{8,9},{9,8},{10,11... | collective-permute-start | bytes 196616 | tf_op jit(solution)/shard_map/ppermute | solution.py:302
  41.6 9.9 %collective-permute-start.3 = (f32[128,128]{1,0:T(8,128)S(1)}, f32[128,128]{1,0:T(8,128)S(1)}, u32[]{:S(2)}, u32[]{:S(2)}) collective-permute-start(f32[128,128]{1,0:T(8,128)S(1)} %get-tuple-element.24.own_ref), channel_id=1, source_target_pairs={{0,7},{1,2},{2,1},{3,4},{4,3},{5,6},{6,5},{7,0},{8,15},{9,10},{10,... | collective-permute-start | bytes 196616 | tf_op jit(solution)/shard_map/ppermute | solution.py:303
  44.8 6.8 %collective-permute-start = (f32[128,128]{1,0:T(8,128)S(1)}, f32[128,128]{1,0:T(8,128)S(1)}, u32[]{:S(2)}, u32[]{:S(2)}) collective-permute-start(f32[128,128]{1,0:T(8,128)S(1)} %get-tuple-element.22), channel_id=1, source_target_pairs={{0,8},{8,0},{16,24},{24,16},{1,9},{9,1},{17,25},{25,17},{2,10},{10... | collective-permute-start | bytes 196616 | tf_op jit(solution)/shard_map/ppermute | solution.py:302
  45.7 5.8 %collective-permute-start.1 = (f32[128,128]{1,0:T(8,128)S(1)}, f32[128,128]{1,0:T(8,128)S(1)}, u32[]{:S(2)}, u32[]{:S(2)}) collective-permute-start(f32[128,128]{1,0:T(8,128)S(1)} %get-tuple-element.23), channel_id=1, source_target_pairs={{0,24},{8,16},{16,8},{24,0},{1,25},{9,17},{17,9},{25,1},{2,26},{10... | collective-permute-start | bytes 196616 | tf_op jit(solution)/shard_map/ppermute | solution.py:303
  60.8 3.4 %collective-permute-start.6 = (f32[128,128]{1,0:T(8,128)S(1)}, f32[128,128]{1,0:T(8,128)S(1)}, u32[]{:S(2)}, u32[]{:S(2)}) collective-permute-start(f32[128,128]{1,0:T(8,128)S(1)} %get-tuple-element.29.own_ref), channel_id=1, source_target_pairs={{0,1},{1,0},{2,3},{3,2},{4,5},{5,4},{6,7},{7,6},{8,9},{9,8},{10,11... | collective-permute-start | bytes 196616 | tf_op jit(solution)/shard_map/ppermute | solution.py:302
  60.8 5.9 %collective-permute-start.7 = (f32[128,128]{1,0:T(8,128)S(1)}, f32[128,128]{1,0:T(8,128)S(1)}, u32[]{:S(2)}, u32[]{:S(2)}) collective-permute-start(f32[128,128]{1,0:T(8,128)S(1)} %get-tuple-element.29.own_ref), channel_id=1, source_target_pairs={{0,7},{1,2},{2,1},{3,4},{4,3},{5,6},{6,5},{7,0},{8,15},{9,10},{10,... | collective-permute-start | bytes 196616 | tf_op jit(solution)/shard_map/ppermute | solution.py:303
  61.1 5.6 %collective-permute-start.4 = (f32[128,128]{1,0:T(8,128)S(1)}, f32[128,128]{1,0:T(8,128)S(1)}, u32[]{:S(2)}, u32[]{:S(2)}) collective-permute-start(f32[128,128]{1,0:T(8,128)S(1)} %get-tuple-element.27), channel_id=1, source_target_pairs={{0,8},{8,0},{16,24},{24,16},{1,9},{9,1},{17,25},{25,17},{2,10},{10... | collective-permute-start | bytes 196616 | tf_op jit(solution)/shard_map/ppermute | solution.py:302
  63.1 3.7 %collective-permute-start.5 = (f32[128,128]{1,0:T(8,128)S(1)}, f32[128,128]{1,0:T(8,128)S(1)}, u32[]{:S(2)}, u32[]{:S(2)}) collective-permute-start(f32[128,128]{1,0:T(8,128)S(1)} %get-tuple-element.28), channel_id=1, source_target_pairs={{0,24},{8,16},{16,8},{24,0},{1,25},{9,17},{17,9},{25,1},{2,26},{10... | collective-permute-start | bytes 196616 | tf_op jit(solution)/shard_map/ppermute | solution.py:303
  66.8 15.5 %copy-start.4 = (s32[2048]{0:T(1024)S(1)}, s32[2048]{0:T(1024)}, u32[]{:S(2)}) copy-start(s32[2048]{0:T(1024)} %param.21) | copy-start | bytes 24580
  75.7 13.1 %collective-permute-start.10 = (f32[128,128]{1,0:T(8,128)S(1)}, f32[128,128]{1,0:T(8,128)S(1)}, u32[]{:S(2)}, u32[]{:S(2)}) collective-permute-start(f32[128,128]{1,0:T(8,128)S(1)} %get-tuple-element.33.own_ref), channel_id=1, source_target_pairs={{0,1},{1,0},{2,3},{3,2},{4,5},{5,4},{6,7},{7,6},{8,9},{9,8},{10,11... | collective-permute-start | bytes 196616 | tf_op jit(solution)/shard_map/ppermute | solution.py:302
  78.6 12.5 %collective-permute-start.11 = (f32[128,128]{1,0:T(8,128)S(1)}, f32[128,128]{1,0:T(8,128)S(1)}, u32[]{:S(2)}, u32[]{:S(2)}) collective-permute-start(f32[128,128]{1,0:T(8,128)S(1)} %get-tuple-element.33.own_ref), channel_id=1, source_target_pairs={{0,7},{1,2},{2,1},{3,4},{4,3},{5,6},{6,5},{7,0},{8,15},{9,10},{10,... | collective-permute-start | bytes 196616 | tf_op jit(solution)/shard_map/ppermute | solution.py:303
  80.6 10.5 %collective-permute-start.8 = (f32[128,128]{1,0:T(8,128)S(1)}, f32[128,128]{1,0:T(8,128)S(1)}, u32[]{:S(2)}, u32[]{:S(2)}) collective-permute-start(f32[128,128]{1,0:T(8,128)S(1)} %get-tuple-element.31), channel_id=1, source_target_pairs={{0,8},{8,0},{16,24},{24,16},{1,9},{9,1},{17,25},{25,17},{2,10},{10... | collective-permute-start | bytes 196616 | tf_op jit(solution)/shard_map/ppermute | solution.py:302
  81.2 10.0 %collective-permute-start.9 = (f32[128,128]{1,0:T(8,128)S(1)}, f32[128,128]{1,0:T(8,128)S(1)}, u32[]{:S(2)}, u32[]{:S(2)}) collective-permute-start(f32[128,128]{1,0:T(8,128)S(1)} %get-tuple-element.32), channel_id=1, source_target_pairs={{0,24},{8,16},{16,8},{24,0},{1,25},{9,17},{17,9},{25,1},{2,26},{10... | collective-permute-start | bytes 196616 | tf_op jit(solution)/shard_map/ppermute | solution.py:303
  84.3 1.3 %collective-permute-start.12 = (f32[8,256]{1,0:T(8,128)S(1)}, f32[8,256]{1,0:T(8,128)S(1)}, u32[]{:S(2)}, u32[]{:S(2)}) collective-permute-start(f32[8,256]{1,0:T(8,128)S(1)} %get-tuple-element.37), channel_id=1, source_target_pairs={{0,8},{8,0},{16,24},{24,16},{1,9},{9,1},{17,25},{25,17},{2,10},{10... | collective-permute-start | bytes 24584 | tf_op jit(solution)/shard_map/ppermute | solution.py:302
  85.7 3.1 %collective-permute-start.13 = (f32[8,256]{1,0:T(8,128)S(1)}, f32[8,256]{1,0:T(8,128)S(1)}, u32[]{:S(2)}, u32[]{:S(2)}) collective-permute-start(f32[8,256]{1,0:T(8,128)S(1)} %get-tuple-element.38), channel_id=1, source_target_pairs={{0,24},{8,16},{16,8},{24,0},{1,25},{9,17},{17,9},{25,1},{2,26},{10... | collective-permute-start | bytes 24584 | tf_op jit(solution)/shard_map/ppermute | solution.py:303
  88.8 9.8 %collective-permute-start.14 = (f32[64,128]{1,0:T(8,128)S(1)}, f32[64,128]{1,0:T(8,128)S(1)}, u32[]{:S(2)}, u32[]{:S(2)}) collective-permute-start(f32[64,128]{1,0:T(8,128)S(1)} %get-tuple-element.40), channel_id=1, source_target_pairs={{0,1},{1,0},{2,3},{3,2},{4,5},{5,4},{6,7},{7,6},{8,9},{9,8},{10,11... | collective-permute-start | bytes 98312 | tf_op jit(solution)/shard_map/ppermute | solution.py:302
  88.8 9.7 %collective-permute-start.15 = (f32[64,128]{1,0:T(8,128)S(1)}, f32[64,128]{1,0:T(8,128)S(1)}, u32[]{:S(2)}, u32[]{:S(2)}) collective-permute-start(f32[64,128]{1,0:T(8,128)S(1)} %get-tuple-element.40), channel_id=1, source_target_pairs={{0,7},{1,2},{2,1},{3,4},{4,3},{5,6},{6,5},{7,0},{8,15},{9,10},{10,... | collective-permute-start | bytes 98312 | tf_op jit(solution)/shard_map/ppermute | solution.py:303
  (2 other events, 1.3 us)

commit v2 on v1

v2 whole, which is shorter than its diff:
```python
import functools

import jax
import jax.numpy as jnp
from jax import lax
from jax.experimental import pallas as pl
from jax.experimental.pallas import tpu as pltpu
from jax.sharding import PartitionSpec as P


MARGIN = 8
HEAT_GAIN = 0.02
SUB = 8
LANES = 128
PIECES = 4
BULKS = 8

VMEM = pl.BlockSpec(memory_space=pltpu.VMEM)
SMEM = pl.BlockSpec(memory_space=pltpu.SMEM)
HBM = pl.BlockSpec(memory_space=pltpu.HBM)


def swap_low(axis):
    return [(i, i ^ 1) for i in range(lax.axis_size(axis))]


def swap_high(axis):
    count = lax.axis_size(axis)
    return [(i, (i + 1 if i % 2 else i - 1) % count) for i in range(count)]


def is_even(axis):
    return lax.rem(lax.axis_index(axis), 2) == 0


def in_hbm(array):
    return pltpu.with_memory_space_constraint(array, pltpu.HBM)


def grant(mebibytes):
    return pltpu.CompilerParams(vmem_limit_bytes=mebibytes * 1024 * 1024)


def cost(flops, nbytes):
    return pl.CostEstimate(flops=flops, bytes_accessed=nbytes, transcendentals=0)


def bulk_copies(pairs, sems, b):
    found = []
    for i, (source, target) in enumerate(pairs):
        deep = source.shape[0] // sems.shape[1]
        at = pl.ds(b * deep, deep)
        target = target.at[at]
        if target.shape != source.at[at].shape:
            target = target.at[:, pl.ds(SUB, source.shape[1])]
        found.append(pltpu.make_async_copy(source.at[at], target, sems.at[i, b]))
    return found


def edge_rows(b, count, i):
    return pl.ds(pl.multiple_of(b * 2 * count, 2 * count) + 2 * i, 2)


def share_edges(axis, edge_a_ref, edge_b_ref, low_ref, high_ref):
    even = is_even(axis)
    edge_a_ref[...] = jnp.where(even, high_ref[...], low_ref[...])
    edge_b_ref[...] = jnp.where(even, low_ref[...], high_ref[...])


def edge_shapes(shape):
    levels, rows, columns = shape
    x = jax.ShapeDtypeStruct((levels * 2, columns), jnp.float32)
    y = jax.ShapeDtypeStruct((levels * rows // LANES * 2, LANES), jnp.float32)
    return x, x, y, y


def edge_scratch(shape):
    return [pltpu.VMEM(edge.shape, edge.dtype) for edge in edge_shapes(shape)]


def keep_edges(b, i, count, fold, rows_of, turned, x_low, x_high, y_low, y_high):
    columns = turned.shape[0]
    for j, rows in enumerate(rows_of):
        x_low[edge_rows(b, count * fold, i * fold + j), :] = rows[0:2]
        x_high[edge_rows(b, count * fold, i * fold + j), :] = rows[-2:]
    y_low[edge_rows(b, count, i), :] = turned[0:2]
    y_high[edge_rows(b, count, i), :] = turned[columns - 2 : columns]


def opening_kernel(
    q_hbm, emitted_hbm, blocks_hbm, source_hbm, live_hbm, xa_ref, xb_ref, ya_ref, yb_ref, sent_hbm,
    x_low, x_high, y_low, y_high, q_ref, emitted_ref, blocks_ref, source_ref, live_ref, light, sent_ref, sems, loaded, done, lit,
):
    levels, rows, columns = q_ref.shape
    bulks = sems.shape[1]
    fold = LANES // rows
    count = levels // bulks // fold

    def copies(b):
        return bulk_copies([(q_hbm, q_ref)], sems, b)

    small = [
        pltpu.make_async_copy(source, target, lit.at[i])
        for i, (source, target) in enumerate(
            ((emitted_hbm, emitted_ref), (source_hbm, source_ref), (live_hbm, live_ref))
        )
    ]
    for copy in small:
        copy.start()
    for b in range(bulks):
        copies(b)[0].start()
    for b in range(loaded.shape[1]):
        bulk_copies([(blocks_hbm, blocks_ref)], loaded, b)[0].start()

    @pl.loop(0, bulks)
    def _(b):
        copies(b)[0].wait()
        for i in range(count):
            q = q_ref[pl.ds((b * count + i) * fold, fold)]
            turned = q.reshape(fold * rows, columns).T
            keep_edges(b, i, count, fold, [q[j] for j in range(fold)], turned, x_low, x_high, y_low, y_high)

    share_edges("gx", xa_ref, xb_ref, x_low, x_high)
    share_edges("gy", ya_ref, yb_ref, y_low, y_high)
    for copy in small:
        copy.wait()
    owned, _, width = light.shape
    for f in range(owned):
        light[f] = emitted_ref[:, f * width : (f + 1) * width].astype(jnp.bfloat16)
    project(
        light, blocks_ref, source_ref, live_ref, sent_hbm, sent_ref, done,
        lambda b: bulk_copies([(blocks_hbm, blocks_ref)], loaded, b)[0].wait(),
    )


def opening(q, emitted, blocks, source, live, message, light):
    return pl.pallas_call(
        opening_kernel,
        out_shape=(*edge_shapes(q.shape), message),
        in_specs=[HBM] * 5,
        out_specs=(*(VMEM,) * 4, HBM),
        scratch_shapes=[
            *edge_scratch(q.shape),
            pltpu.VMEM(q.shape, jnp.float32),
            pltpu.VMEM(emitted.shape, jnp.float32),
            pltpu.VMEM(blocks.shape, jnp.bfloat16),
            pltpu.SMEM(source.shape, jnp.int32),
            pltpu.SMEM(live.shape, jnp.int32),
            light,
            pltpu.VMEM(message.shape, jnp.float32),
            pltpu.SemaphoreType.DMA((1, BULKS)),
            pltpu.SemaphoreType.DMA((1, PIECES)),
            pltpu.SemaphoreType.DMA((PIECES,)),
            pltpu.SemaphoreType.DMA((3,)),
        ],
        name="opening",
        compiler_params=grant(8 + 5 * blocks.shape[0] // 32),
        cost_estimate=cost(12_000_000, q.size * 4 + blocks.size * 2),
    )(*map(in_hbm, (q, emitted, blocks, source, live)))


def moved(back_two, back, center, ahead, ahead_two, velocity):
    positive = velocity >= 0.0
    near = jnp.where(positive, back, ahead)
    far = jnp.where(positive, back_two, ahead_two)
    return jnp.abs(velocity) * ((far - 8.0 * near) + (2.0 * (back + ahead) + 3.0 * center))


def stage_kernel(
    coefficient, first_stage, last, begin, end, base_hbm, q_hbm, e_hbm, n_hbm, u_hbm,
    xa_in, xb_in, ya_in, yb_in, *rest,
):
    if begin > 0:
        _, *rest = rest
    out_hbm, *rest = rest
    if last:
        if begin == 0:
            ground_ref, *rest = rest
    else:
        xa_ref, xb_ref, ya_ref, yb_ref, *rest = rest
    if first_stage:
        speed_hbm, *rest = rest
    x_low, x_high, y_low, y_high, padded, turned, base_ref, e_ref, n_ref, u_ref, out_ref, *rest = rest
    speed_ref = n_ref
    if first_stage:
        speed_ref, *rest = rest
    sems, done = rest
    levels, rows, columns = out_ref.shape
    tiles = rows // SUB
    bulks = sems.shape[1]
    fold = LANES // rows
    count = levels // bulks // fold

    def field(b):
        return bulk_copies([(q_hbm, padded)], sems, b)

    def others(b):
        found = [(e_hbm, e_ref), (n_hbm, n_ref), (u_hbm, u_ref)]
        if not first_stage:
            found.append((base_hbm, base_ref))
        return bulk_copies([(q_hbm, padded)] + found, sems, b)[1:]

    def outgoing(b):
        found = [(out_ref, out_hbm)]
        if first_stage:
            found.append((speed_ref, speed_hbm))
        return bulk_copies(found, done, b)

    below, above = max(begin - 1, 0), min(end + 1, bulks)
    for b in range(below, above):
        for copy in field(b):
            copy.start()
    for b in range(begin, end):
        for copy in others(b):
            copy.start()
    even_x, even_y = is_even("gx"), is_even("gy")

    @pl.loop(begin, end)
    def _(b):
        for copy in field(b):
            copy.wait()
        for i in range(count):
            p = b * count + i
            for j in range(fold):
                level = p * fold + j
                at = edge_rows(b, count * fold, i * fold + j)
                got_a, got_b = xa_in[at, :], xb_in[at, :]
                padded[level, SUB - 2 : SUB, :] = jnp.where(even_x, got_b, got_a)
                padded[level, SUB + rows : SUB + rows + 2, :] = jnp.where(even_x, got_a, got_b)
            at = edge_rows(b, count, i)
            got_a, got_b = ya_in[at, :], yb_in[at, :]
            turned[p, SUB - 2 : SUB, :] = jnp.where(even_y, got_b, got_a)
            turned[p, SUB + columns : SUB + columns + 2, :] = jnp.where(even_y, got_a, got_b)
            q = padded[pl.ds(p * fold, fold), SUB : SUB + rows, :]
            turned[p, SUB : SUB + columns, :] = q.reshape(fold * rows, columns).T

    for b in [*range(below, begin), *range(end, above)]:
        for copy in field(b):
            copy.wait()

    @pl.loop(begin, end)
    def _(b):
        for copy in others(b):
            copy.wait()
        for i in range(count):
            p = b * count + i
            if first_stage:
                speed_ref[p] = n_ref[pl.ds(p * fold, fold)].reshape(fold * rows, columns).T
            terms = []
            for t in range(columns // SUB):

                def line(offset):
                    return turned[p, SUB + t * SUB + offset : 2 * SUB + t * SUB + offset, :]

                terms.append(
                    moved(line(-2), line(-1), line(0), line(1), line(2), speed_ref[p, t * SUB : (t + 1) * SUB, :])
                )
            along_y = jnp.concatenate(terms, axis=0).T
            results = [[] for _ in range(fold)]
            for t in range(tiles):
                tile = slice(t * SUB, (t + 1) * SUB)
                column = []
                for d in range(-2, fold + 2):
                    level = p * fold + d
                    if i * fold + d < 0:
                        level = jnp.maximum(level, 0)
                    elif i * fold + d >= count * fold:
                        level = jnp.minimum(level, levels - 1)
                    column.append(padded[level, SUB + t * SUB : 2 * SUB + t * SUB, :])
                for j in range(fold):
                    level = p * fold + j

                    def row(offset):
                        return padded[level, SUB + t * SUB + offset : 2 * SUB + t * SUB + offset, :]

                    q = column[j + 2]
                    total = moved(row(-2), row(-1), q, row(1), row(2), e_ref[level, tile, :])
                    total += moved(*column[j : j + 5], u_ref[level, tile, :])
                    total += along_y[j * rows + t * SUB : j * rows + (t + 1) * SUB]
                    base = q if first_stage else base_ref[level, tile, :]
                    result = base - (coefficient / 6.0) * total
                    out_ref[level, tile, :] = result
                    results[j].append(result)
            if not last:
                found = [jnp.concatenate(part, axis=0) for part in results]
                keep_edges(
                    b, i, count, fold, found, jnp.concatenate(found, axis=0).T, x_low, x_high, y_low, y_high
                )
        for copy in outgoing(b):
            copy.start()

    if last:
        if begin == 0:
            ground_ref[...] = out_ref[0]
    else:
        share_edges("gx", xa_ref, xb_ref, x_low, x_high)
        share_edges("gy", ya_ref, yb_ref, y_low, y_high)
    for b in range(begin, end):
        for copy in outgoing(b):
            copy.wait()


def stage(base, q, winds, edges, coefficient, first_stage=False, last=False, begin=0, end=BULKS, started=None):
    levels, rows, columns = q.shape
    blocks = levels * rows // LANES
    whole = pltpu.HBM(q.shape, jnp.float32)
    ground = jax.ShapeDtypeStruct((rows, columns), jnp.float32)
    outs = (whole, *(() if last else edge_shapes(q.shape)))
    outs += (ground,) if last and begin == 0 else ()
    outs += (pltpu.HBM((blocks, columns, LANES), jnp.float32),) if first_stage else ()
    field = pltpu.VMEM(q.shape, jnp.float32)
    turned = pltpu.VMEM((blocks, columns, LANES), jnp.float32)
    return pl.pallas_call(
        functools.partial(stage_kernel, coefficient, first_stage, last, begin, end),
        out_shape=outs,
        in_specs=[HBM] * 5 + [VMEM] * 4 + [HBM] * (begin > 0),
        input_output_aliases={9: 0} if begin > 0 else {},
        out_specs=tuple(HBM if isinstance(out, type(whole)) else VMEM for out in outs),
        scratch_shapes=[
            *edge_scratch(q.shape),
            pltpu.VMEM((levels, rows + 2 * SUB, columns), jnp.float32),
            pltpu.VMEM((blocks, columns + 2 * SUB, LANES), jnp.float32),
            pltpu.VMEM((SUB, LANES), jnp.float32) if first_stage else field,
            field,
            field if first_stage else turned,
            field,
            field,
            *([turned] if first_stage else []),
            pltpu.SemaphoreType.DMA((5, BULKS)),
            pltpu.SemaphoreType.DMA((2, BULKS)),
        ],
        name="stage",
        compiler_params=grant(20),
        cost_estimate=cost(24_000_000 * (end - begin) // BULKS, q.size * 24 * (end - begin) // BULKS),
    )(*map(in_hbm, (base, q, *winds)), *edges, *([started] if begin > 0 else []))


def swap(array, axis):
    a = lax.ppermute(array[0], axis, swap_low(axis))
    b = lax.ppermute(array[1], axis, swap_high(axis))
    return a, b


def neighbours(x_low, x_high, y_low, y_high):
    y_edges = swap((y_low, y_high), "gy")
    x_edges = swap((x_low, x_high), "gx")
    return *x_edges, *y_edges


def exchange(sent):
    return lax.all_to_all(sent, ("gx", "gy"), split_axis=0, concat_axis=0, tiled=True)


def project(light, blocks_ref, source_ref, live_ref, sent_hbm, sent_ref, done, ready=None):
    peers, slots, width, _ = blocks_ref.shape
    bands = light.shape[1]
    nothing = jnp.zeros((bands, width), jnp.bfloat16)
    pieces = done.shape[0]
    share = peers // pieces

    def outgoing(p):
        at = pl.ds(p * share, share)
        return pltpu.make_async_copy(sent_ref.at[at], sent_hbm.at[at], done.at[p])

    for p in range(pieces):
        if ready is not None:
            ready(p)

        @pl.loop(p * share, (p + 1) * share, unroll=4)
        def _(r):
            for c in range(0, slots, 2):
                one = light[source_ref[c, r]]
                two = light[source_ref[c + 1, r]]
                left = jnp.concatenate(
                    [jnp.concatenate([one, nothing], axis=1), jnp.concatenate([nothing, two], axis=1)], axis=0
                )
                right = blocks_ref[r, c : c + 2].reshape(2 * width, width)
                got = jnp.dot(left, right, preferred_element_type=jnp.float32)
                for d in range(2):
                    scale = jnp.where(c + d < live_ref[0, r], 0.5 / width, 0.0)
                    sent_ref[r, c + d] = got[d * bands : (d + 1) * bands] * scale

        outgoing(p).start()
    for p in range(pieces):
        outgoing(p).wait()


def gather_light(arrived_ref, target_ref, total):
    peers, slots = arrived_ref.shape[:2]
    total[...] = jnp.zeros_like(total)

    @pl.loop(0, peers, unroll=4)
    def _(s):
        for c in range(slots):
            g = target_ref[c, s]
            total[g] = total[g] + arrived_ref[s, c]


def second_kernel(
    arrived_ref, target_ref, emitted_ref, albedo_ref, blocks_hbm, source_ref, live_ref, sent_hbm,
    light, total, blocks_ref, sent_ref, done, loaded,
):
    pieces = loaded.shape[0]
    share = blocks_ref.shape[0] // pieces

    def incoming(p):
        at = pl.ds(p * share, share)
        return pltpu.make_async_copy(blocks_hbm.at[at], blocks_ref.at[at], loaded.at[p])

    for p in range(pieces):
        incoming(p).start()
    gather_light(arrived_ref, target_ref, total)
    blocks, _, width = light.shape
    for f in range(blocks):
        at = slice(f * width, (f + 1) * width)
        light[f] = (emitted_ref[:, at] + albedo_ref[:, at] * total[f]).astype(jnp.bfloat16)
    project(light, blocks_ref, source_ref, live_ref, sent_hbm, sent_ref, done, lambda p: incoming(p).wait())


def last_kernel(
    rows, columns, arrived_ref, target_ref, emitted_ref, albedo_ref, ground_ref,
    leaving_ref, inner_ref, rim_a_ref, rim_b_ref, total, heat, cells,
):
    gather_light(arrived_ref, target_ref, total)
    blocks, _, width = total.shape
    span_x, span_y = rows + 2 * MARGIN, columns + 2 * MARGIN
    x_index = lax.broadcasted_iota(jnp.int32, (span_x, width), 0).astype(jnp.float32)
    y_index = lax.broadcasted_iota(jnp.int32, (2 * columns, width), 0).astype(jnp.float32)
    for f in range(blocks):
        at = slice(f * width, (f + 1) * width)
        light = total[f]
        albedo = albedo_ref[:, at]
        leaving_ref[:, at] = emitted_ref[:, at] + albedo * light
        absorbed = HEAT_GAIN * jnp.sum((1.0 - albedo) * light, axis=0, keepdims=True)
        place = ground_ref[f : f + 1, :].astype(jnp.float32)
        x = jnp.floor((place + 0.5) * (1.0 / span_y))
        y = place - span_y * x
        x = jnp.where(x < MARGIN, x + (span_x - MARGIN), x - MARGIN)
        y = jnp.where(y < MARGIN, y + (2 * columns - MARGIN), y - MARGIN)
        coarse = absorbed.astype(jnp.bfloat16).astype(jnp.float32)
        fine = absorbed - coarse
        hit = x_index == x
        heat[0:span_x, at] = jnp.where(hit, coarse, 0.0).astype(jnp.bfloat16)
        heat[span_x : 2 * span_x, at] = jnp.where(hit, fine, 0.0).astype(jnp.bfloat16)
        cells[:, at] = jnp.where(y_index == y, 1.0, 0.0).astype(jnp.bfloat16)
    both = lax.dot_general(
        heat[...], cells[...], (((1,), (1,)), ((), ())), preferred_element_type=jnp.float32
    )
    field = both[0:span_x] + both[span_x : 2 * span_x]
    inner_ref[...] = field[0:rows]
    upper = field[rows : rows + MARGIN]
    lower = field[rows + MARGIN : rows + 2 * MARGIN]
    even = is_even("gx")
    rim_a_ref[...] = jnp.where(even, upper, lower)
    rim_b_ref[...] = jnp.where(even, lower, upper)


def fold_kernel(inner_ref, rim_a_ref, rim_b_ref, middle_ref, side_ref):
    rows, columns = middle_ref.shape
    even = is_even("gx")
    for half, ref in ((0, middle_ref), (1, side_ref)):
        at = slice(half * columns, (half + 1) * columns)
        rim_a, rim_b = rim_a_ref[:, at], rim_b_ref[:, at]
        ref[...] = inner_ref[:, at]
        ref[0:MARGIN, :] = ref[0:MARGIN, :] + jnp.where(even, rim_b, rim_a)
        ref[rows - MARGIN : rows, :] = ref[rows - MARGIN : rows, :] + jnp.where(even, rim_a, rim_b)


def finish_kernel(field_ref, ground_ref, middle_ref, side_a_ref, side_b_ref, out_ref, level, sem):
    lane = lax.broadcasted_iota(jnp.int32, level.shape, 1)
    columns = level.shape[1]
    even = is_even("gy")
    left = jnp.where(even, side_b_ref[...], side_a_ref[...])
    right = jnp.where(even, side_a_ref[...], side_b_ref[...])
    level[...] = (
        ground_ref[...]
        + middle_ref[...]
        + jnp.where(lane < MARGIN, left, 0.0)
        + jnp.where(lane >= columns - MARGIN, right, 0.0)
    )
    copy = pltpu.make_async_copy(level, out_ref.at[0], sem)
    copy.start()
    copy.wait()


def step(
    thermal_anomaly,
    eastward_shift_ratio,
    northward_shift_ratio,
    upward_shift_ratio,
    emitted_power,
    albedo_values,
    visibility_matrices,
    active_pairing_totals,
    sender_panel_group,
    receiver_panel_group,
    nearest_ground_index,
):
    _, rows, columns = thermal_anomaly.shape
    bands, faces = emitted_power.shape
    blocks = visibility_matrices[0]
    peers, slots, width, _ = blocks.shape
    owned = faces // width
    source = jnp.transpose(sender_panel_group[0])
    target = jnp.transpose(receiver_panel_group[:, 0, :])
    message = pltpu.HBM((peers, slots, bands, width), jnp.float32)
    light = pltpu.VMEM((owned, bands, width), jnp.bfloat16)
    total = pltpu.VMEM((owned, bands, width), jnp.float32)
    winds = (eastward_shift_ratio, northward_shift_ratio, upward_shift_ratio)

    *edges, sent = opening(
        thermal_anomaly, emitted_power, blocks, source, active_pairing_totals, message, light
    )
    edges = neighbours(*edges)
    arrived = exchange(sent)

    one, *sides, speed = stage(thermal_anomaly, thermal_anomaly, winds, edges, 1.0 / 3.0, first_stage=True)
    winds = (eastward_shift_ratio, speed, upward_shift_ratio)
    edges = neighbours(*sides)

    sent = pl.pallas_call(
        second_kernel,
        out_shape=message,
        in_specs=[VMEM, SMEM, VMEM, VMEM, HBM, SMEM, SMEM],
        out_specs=HBM,
        scratch_shapes=[
            light,
            total,
            pltpu.VMEM(blocks.shape, jnp.bfloat16),
            pltpu.VMEM(message.shape, jnp.float32),
            pltpu.SemaphoreType.DMA((PIECES,)),
            pltpu.SemaphoreType.DMA((PIECES,)),
        ],
        name="second",
        compiler_params=grant(6 + 6 * peers // 32),
        cost_estimate=cost(12_000_000, blocks.size * 2),
    )(arrived, target, emitted_power, albedo_values, in_hbm(blocks), source, active_pairing_totals)
    arrived = exchange(sent)

    two, *sides = stage(thermal_anomaly, one, winds, edges, 1.0 / 2.0)
    edges = neighbours(*sides)

    span_x = rows + 2 * MARGIN
    rim = jax.ShapeDtypeStruct((MARGIN, 2 * columns), jnp.float32)
    leaving, inner, *rims = pl.pallas_call(
        functools.partial(last_kernel, rows, columns),
        out_shape=(
            jax.ShapeDtypeStruct((bands, faces), jnp.float32),
            jax.ShapeDtypeStruct((rows, 2 * columns), jnp.float32),
            rim,
            rim,
        ),
        in_specs=[VMEM, SMEM, VMEM, VMEM, VMEM],
        out_specs=(VMEM,) * 4,
        scratch_shapes=[
            total,
            pltpu.VMEM((2 * span_x, faces), jnp.bfloat16),
            pltpu.VMEM((2 * columns, faces), jnp.bfloat16),
        ],
        name="last",
        compiler_params=grant(8),
        cost_estimate=cost(16_000_000, arrived.size * 4),
    )(arrived, target, emitted_power, albedo_values, nearest_ground_index.reshape(owned, width))
    rims = swap(rims, "gx")

    three, ground = stage(thermal_anomaly, two, winds, edges, 1.0, last=True)

    flat = jax.ShapeDtypeStruct((rows, columns), jnp.float32)
    middle, side = pl.pallas_call(
        fold_kernel,
        out_shape=(flat, flat),
        in_specs=[VMEM] * 3,
        out_specs=(VMEM, VMEM),
        name="fold",
        compiler_params=grant(2),
        cost_estimate=cost(500_000, flat.size * 8),
    )(inner, *rims)
    sides = swap((side, side), "gy")

    renewed = pl.pallas_call(
        finish_kernel,
        out_shape=jax.ShapeDtypeStruct(thermal_anomaly.shape, jnp.float32),
        in_specs=[HBM, VMEM, VMEM, VMEM, VMEM],
        out_specs=HBM,
        scratch_shapes=[pltpu.VMEM((rows, columns), jnp.float32), pltpu.SemaphoreType.DMA],
        input_output_aliases={0: 0},
        name="finish",
        compiler_params=grant(2),
        cost_estimate=cost(500_000, flat.size * 8),
    )(three, ground, middle, *sides)
    return renewed, leaving


def solution(mesh):
    in_specs = (
        P(None, "gx", "gy"),
        P(None, "gx", "gy"),
        P(None, "gx", "gy"),
        P(None, "gx", "gy"),
        P(None, ("gx", "gy")),
        P(None, ("gx", "gy")),
        P(("gx", "gy"), None, None, None, None),
        P(("gx", "gy"), None),
        P(("gx", "gy"), None, None),
        P(None, ("gx", "gy"), None),
        P(("gx", "gy")),
    )
    out_specs = (P(None, "gx", "gy"), P(None, ("gx", "gy")))
    return jax.shard_map(step, mesh=mesh, in_specs=in_specs, out_specs=out_specs, check_vma=False)
```

time: 100 us -> 90.1 us (0.901)
  the two profiles are of different devices: /device:TPU:1 before, /device:TPU:0 now
where the time goes in v2:
time: 90.1 us; the launch traced here: 89.8 us
  Pallas kernels  30.6 us (34%)
  blocking collectives  23.6 us (26%)
  starting transfers between devices  18.7 us (21%)
  waiting for transfers between devices  16.1 us (18%)
    all_to_all x1, blocking collectives, exchange(): lax.all_to_all(sent, ('gx', 'gy'), split_axis=0, concat_axis=0, tiled=True)  23.6 us
    pallas_call x3, Pallas kernels, stage(): pl.pallas_call(functools.partial(stage_kernel, coefficient, first_stage,...  19.7 us
    ppermute x8, starting transfers between devices, swap(): b = lax.ppermute(array[1], axis, swap_high(axis))  14.1 us
    ppermute x8, waiting for transfers between devices, swap(): b = lax.ppermute(array[1], axis, swap_high(axis))  12.5 us
    pallas_call x1, Pallas kernels, opening(): pl.pallas_call(opening_kernel, out_shape=(*edge_shapes(q.shape), message)...  4.5 us
    pallas_call x1, Pallas kernels, step(): pl.pallas_call(second_kernel, out_shape=message, in_specs=[VMEM, SMEM, VM...  3.69 us
    ppermute x8, waiting for transfers between devices, swap(): a = lax.ppermute(array[0], axis, swap_low(axis))  3.59 us
    all_to_all x1, starting transfers between devices, exchange(): lax.all_to_all(sent, ('gx', 'gy'), split_axis=0, concat_axis=0, tiled=True)  2.62 us
  transfers between devices with their start and end apart: 17, of which 4 were waited for; matrix products, arithmetic and copies ran while one was open for 0% of the time, Pallas kernels for 24%

profile of v2, /device:TPU:0, one launch (start us, length us, event | category | flops | bytes accessed | tf_op | source)
XLA Modules:
  0.0 89.8 jit_solution(580957297243038411)
XLA Ops:
  0.7 4.5 %opening.1 = (f32[128,128]{1,0:T(8,128)S(1)}, f32[128,128]{1,0:T(8,128)S(1)}, f32[64,128]{1,0:T(8,128)S(1)}, f32[64,128]{1,0:T(8,128)S(1)}, f32[32,2,16,128]{3,2,1,0:T(8,128)}) custom-call(f32[64,64,128]{2,1,0:T(8,128)} %base_hbm.5, f32[16,2048]{1,0:T(8,128)} %emitted_ref.3, bf16[32,2,128,128]{3,2,1,0:T(8,128)(2,1)} %bitcast.13, s32[2,32]{1,0:T(2,128)} %bitcast.9, ...), custom_call_target="tpu_custom_call" | custom-call | flops 12000000 | bytes 4194304 | tf_op jit(solution)/shard_map/opening/pallas_call | solution.py:137
  5.2 23.6 %all_to_all.10.arrived_ref = f32[32,2,16,128]{3,2,1,0:T(8,128)S(1)} all-to-all(f32[32,2,16,128]{3,2,1,0:T(8,128)} %get-tuple-element.43), channel_id=1, replica_groups=mesh['gx'=4,'gy'=8] {'gx','gy'}, dimensions={0} | all-to-all | bytes 1048576 | tf_op jit(solution)/shard_map/all_to_all | solution.py:351
  28.8 3.7 %second.1 = f32[32,2,16,128]{3,2,1,0:T(8,128)} custom-call(f32[32,2,16,128]{3,2,1,0:T(8,128)S(1)} %all_to_all.10.arrived_ref, s32[2,32]{1,0:T(2,128)S(1)} %bitcast.11, f32[16,2048]{1,0:T(8,128)S(1)} %copy-done, f32[16,2048]{1,0:T(8,128)S(1)} %copy-done.1, bf16[32,2,128,128]{3,2,1,0:T(8,128)(2,1)} %bitcast.14, s32[2,32]{1,0:T(2,128)S(1)} %bitcast.10, ...), custom_call_target="tpu_custom_call" | custom-call | flops 12000000 | bytes 2097152 | tf_op jit(solution)/shard_map/second/pallas_call | solution.py:521
  32.5 2.6 %all-to-all-start.1 = ((f32[32,2,16,128]{3,2,1,0:T(8,128)}), f32[32,2,16,128]{3,2,1,0:T(8,128)S(1)}, u32[]{:S(2)}, u32[]{:S(2)}) async-start(f32[32,2,16,128]{3,2,1,0:T(8,128)} %second.1), calls=%async_computation.1 | async-start | bytes 1048576 | tf_op jit(solution)/shard_map/all_to_all | solution.py:351
  35.1 0.2 collective-permute-start
  35.3 1.7 %collective-permute-start.1 = (f32[128,128]{1,0:T(8,128)S(1)}, f32[128,128]{1,0:T(8,128)S(1)}, u32[]{:S(2)}, u32[]{:S(2)}) collective-permute-start(f32[128,128]{1,0:T(8,128)S(1)} %get-tuple-element.27), channel_id=1, source_target_pairs={{0,24},{8,16},{16,8},{24,0},{1,25},{9,17},{17,9},{25,1},{2,26},{10... | collective-permute-start | bytes 196616 | tf_op jit(solution)/shard_map/ppermute | solution.py:340
  37.0 1.5 %collective-permute-start.2 = (f32[64,128]{1,0:T(8,128)S(1)}, f32[64,128]{1,0:T(8,128)S(1)}, u32[]{:S(2)}, u32[]{:S(2)}) collective-permute-start(f32[64,128]{1,0:T(8,128)S(1)} %get-tuple-element.28), channel_id=1, source_target_pairs={{0,1},{1,0},{2,3},{3,2},{4,5},{5,4},{6,7},{7,6},{8,9},{9,8},{10,11... | collective-permute-start | bytes 98312 | tf_op jit(solution)/shard_map/ppermute | solution.py:339
  38.4 3.4 %collective-permute-start.3 = (f32[64,128]{1,0:T(8,128)S(1)}, f32[64,128]{1,0:T(8,128)S(1)}, u32[]{:S(2)}, u32[]{:S(2)}) collective-permute-start(f32[64,128]{1,0:T(8,128)S(1)} %get-tuple-element.29), channel_id=1, source_target_pairs={{0,7},{1,2},{2,1},{3,4},{4,3},{5,6},{6,5},{7,0},{8,15},{9,10},{10,... | collective-permute-start | bytes 98312 | tf_op jit(solution)/shard_map/ppermute | solution.py:340
  41.9 8.0 %collective-permute-done.3.yb_in = f32[64,128]{1,0:T(8,128)S(1)} collective-permute-done((f32[64,128]{1,0:T(8,128)S(1)}, f32[64,128]{1,0:T(8,128)S(1)}, u32[]{:S(2)}, u32[]{:S(2)}) %collective-permute-start.3) | collective-permute-done | bytes 32800 | tf_op jit(solution)/shard_map/ppermute | solution.py:340
  49.9 7.0 %stage.3 = (f32[64,64,128]{2,1,0:T(8,128)}, f32[128,128]{1,0:T(8,128)S(1)}, f32[128,128]{1,0:T(8,128)S(1)}, f32[64,128]{1,0:T(8,128)S(1)}, f32[64,128]{1,0:T(8,128)S(1)}, /*index=5*/f32[32,128,128]{2,1,0:T(8,128)}) custom-call(f32[64,64,128]{2,1,0:T(8,128)} %base_hbm.5, f32[64,64,128]{2,1,0:T(8,128)} %base_hbm.5, f32[64,64,128]{2,1,0:T(8,128)} %e_hbm.5, ...), custom_call_target="tpu_custom_call" | custom-call | flops 24000000 | bytes 12582912 | tf_op jit(solution)/shard_map/stage/pallas_call | solution.py:313
  57.0 1.6 %collective-permute-start.5 = (f32[128,128]{1,0:T(8,128)S(1)}, f32[128,128]{1,0:T(8,128)S(1)}, u32[]{:S(2)}, u32[]{:S(2)}) collective-permute-start(f32[128,128]{1,0:T(8,128)S(1)} %get-tuple-element.33), channel_id=1, source_target_pairs={{0,24},{8,16},{16,8},{24,0},{1,25},{9,17},{17,9},{25,1},{2,26},{10... | collective-permute-start | bytes 196616 | tf_op jit(solution)/shard_map/ppermute | solution.py:340
  58.6 0.3 collective-permute-start.7
  58.9 3.6 %collective-permute-done.6.ya_in = f32[64,128]{1,0:T(8,128)S(1)} collective-permute-done((f32[64,128]{1,0:T(8,128)S(1)}, f32[64,128]{1,0:T(8,128)S(1)}, u32[]{:S(2)}, u32[]{:S(2)}) %collective-permute-start.6) | collective-permute-done | bytes 32800 | tf_op jit(solution)/shard_map/ppermute | solution.py:339
  62.5 2.7 %collective-permute-done.7.yb_in = f32[64,128]{1,0:T(8,128)S(1)} collective-permute-done((f32[64,128]{1,0:T(8,128)S(1)}, f32[64,128]{1,0:T(8,128)S(1)}, u32[]{:S(2)}, u32[]{:S(2)}) %collective-permute-start.7) | collective-permute-done | bytes 32800 | tf_op jit(solution)/shard_map/ppermute | solution.py:340
  65.2 6.6 %stage.4 = (f32[64,64,128]{2,1,0:T(8,128)}, f32[128,128]{1,0:T(8,128)S(1)}, f32[128,128]{1,0:T(8,128)S(1)}, f32[64,128]{1,0:T(8,128)S(1)}, f32[64,128]{1,0:T(8,128)S(1)}) custom-call(f32[64,64,128]{2,1,0:T(8,128)} %base_hbm.5, f32[64,64,128]{2,1,0:T(8,128)} %get-tuple-element.30.q_hbm, f32[64,64,128]{2,1,0:T(8,128)} %e_hbm.5, ...), custom_call_target="tpu_custom_call" | custom-call | flops 24000000 | bytes 12582912 | tf_op jit(solution)/shard_map/stage/pallas_call | solution.py:313
  71.8 0.6 collective-permute-start.9
  72.5 0.2 collective-permute-start.10
  72.7 2.1 %last.1 = (f32[16,2048]{1,0:T(8,128)}, f32[64,256]{1,0:T(8,128)S(1)}, f32[8,256]{1,0:T(8,128)S(1)}, f32[8,256]{1,0:T(8,128)S(1)}) custom-call(f32[32,2,16,128]{3,2,1,0:T(8,128)S(1)} %all-to-all-done.1.arrived_ref, s32[2,32]{1,0:T(2,128)S(1)} %bitcast.12, f32[16,2048]{1,0:T(8,128)S(1)} %copy-done, f32[16,2048]{1,0:T(8,128)S(1)} %copy-done.1, ...), custom_call_target="tpu_custom_call" | custom-call | flops 16000000 | bytes 524288 | tf_op jit(solution)/shard_map/last/pallas_call | solution.py:545
  74.8 1.6 %collective-permute-start.13 = (f32[8,256]{1,0:T(8,128)S(1)}, f32[8,256]{1,0:T(8,128)S(1)}, u32[]{:S(2)}, u32[]{:S(2)}) collective-permute-start(f32[8,256]{1,0:T(8,128)S(1)} %get-tuple-element.46), channel_id=1, source_target_pairs={{0,24},{8,16},{16,8},{24,0},{1,25},{9,17},{17,9},{25,1},{2,26},{10... | collective-permute-start | bytes 24584 | tf_op jit(solution)/shard_map/ppermute | solution.py:340
  76.4 1.7 %collective-permute-start.11 = (f32[64,128]{1,0:T(8,128)S(1)}, f32[64,128]{1,0:T(8,128)S(1)}, u32[]{:S(2)}, u32[]{:S(2)}) collective-permute-start(f32[64,128]{1,0:T(8,128)S(1)} %get-tuple-element.40), channel_id=1, source_target_pairs={{0,7},{1,2},{2,1},{3,4},{4,3},{5,6},{6,5},{7,0},{8,15},{9,10},{10,... | collective-permute-start | bytes 98312 | tf_op jit(solution)/shard_map/ppermute | solution.py:340
  78.1 3.1 %collective-permute-start.15 = (f32[64,128]{1,0:T(8,128)S(1)}, f32[64,128]{1,0:T(8,128)S(1)}, u32[]{:S(2)}, u32[]{:S(2)}) collective-permute-start(f32[64,128]{1,0:T(8,128)S(1)} %get-tuple-element.48), channel_id=1, source_target_pairs={{0,7},{1,2},{2,1},{3,4},{4,3},{5,6},{6,5},{7,0},{8,15},{9,10},{10,... | collective-permute-start | bytes 98312 | tf_op jit(solution)/shard_map/ppermute | solution.py:340
  81.2 1.8 %collective-permute-done.11.yb_in = f32[64,128]{1,0:T(8,128)S(1)} collective-permute-done((f32[64,128]{1,0:T(8,128)S(1)}, f32[64,128]{1,0:T(8,128)S(1)}, u32[]{:S(2)}, u32[]{:S(2)}) %collective-permute-start.11) | collective-permute-done | bytes 32800 | tf_op jit(solution)/shard_map/ppermute | solution.py:340
  83.0 6.1 %stage.5 = (f32[64,64,128]{2,1,0:T(8,128)}, f32[64,128]{1,0:T(8,128)S(1)}) custom-call(f32[64,64,128]{2,1,0:T(8,128)} %base_hbm.5, f32[64,64,128]{2,1,0:T(8,128)} %get-tuple-element.36.q_hbm, f32[64,64,128]{2,1,0:T(8,128)} %e_hbm.5, f32[32,128,128]{2,1,0:T(8,128)} %get-tuple-element.31.n_hbm, f32[64,64,128]{2,1,0:T(8,128)} %u_hbm.5, ...), custom_call_target="tpu_custom_call" | custom-call | flops 24000000 | bytes 12582912 | tf_op jit(solution)/shard_map/stage/pallas_call | solution.py:313
  89.1 0.6 finish.1
  (31 shorter events, 0.2 us)
Async XLA Ops:
  0.6 28.1 %copy-start = (f32[16,2048]{1,0:T(8,128)S(1)}, f32[16,2048]{1,0:T(8,128)}, u32[]{:S(2)}) copy-start(f32[16,2048]{1,0:T(8,128)} %emitted_ref.3) | copy-start | bytes 393220
  0.6 28.1 %copy-start.1 = (f32[16,2048]{1,0:T(8,128)S(1)}, f32[16,2048]{1,0:T(8,128)}, u32[]{:S(2)}) copy-start(f32[16,2048]{1,0:T(8,128)} %albedo_ref.3) | copy-start | bytes 393220
  0.7 28.1 %copy-start.3 = (s32[1,32,2]{1,2,0:T(2,128)S(1)}, s32[1,32,2]{1,2,0:T(2,128)}, u32[]{:S(2)}) copy-start(s32[1,32,2]{1,2,0:T(2,128)} %param.19) | copy-start | bytes 772
  0.7 28.1 %copy-start.4 = (s32[32,1,2]{0,2,1:T(2,128)S(1)}, s32[32,1,2]{0,2,1:T(2,128)}, u32[]{:S(2)}) copy-start(s32[32,1,2]{0,2,1:T(2,128)} %param.20) | copy-start | bytes 772
  0.7 28.1 %copy-start.5 = (s32[1,32]{1,0:T(1,128)S(1)}, s32[1,32]{1,0:T(1,128)}, u32[]{:S(2)}) copy-start(s32[1,32]{1,0:T(1,128)} %live_ref.1) | copy-start | bytes 388
  32.5 40.2 %all-to-all-start.1 = ((f32[32,2,16,128]{3,2,1,0:T(8,128)}), f32[32,2,16,128]{3,2,1,0:T(8,128)S(1)}, u32[]{:S(2)}, u32[]{:S(2)}) async-start(f32[32,2,16,128]{3,2,1,0:T(8,128)} %second.1), calls=%async_computation.1 | async-start | bytes 1048576 | tf_op jit(solution)/shard_map/all_to_all | solution.py:351
  35.1 14.7 %collective-permute-start = (f32[128,128]{1,0:T(8,128)S(1)}, f32[128,128]{1,0:T(8,128)S(1)}, u32[]{:S(2)}, u32[]{:S(2)}) collective-permute-start(f32[128,128]{1,0:T(8,128)S(1)} %get-tuple-element.26), channel_id=1, source_target_pairs={{0,8},{8,0},{16,24},{24,16},{1,9},{9,1},{17,25},{25,17},{2,10},{10... | collective-permute-start | bytes 196616 | tf_op jit(solution)/shard_map/ppermute | solution.py:339
  35.3 14.6 %collective-permute-start.1 = (f32[128,128]{1,0:T(8,128)S(1)}, f32[128,128]{1,0:T(8,128)S(1)}, u32[]{:S(2)}, u32[]{:S(2)}) collective-permute-start(f32[128,128]{1,0:T(8,128)S(1)} %get-tuple-element.27), channel_id=1, source_target_pairs={{0,24},{8,16},{16,8},{24,0},{1,25},{9,17},{17,9},{25,1},{2,26},{10... | collective-permute-start | bytes 196616 | tf_op jit(solution)/shard_map/ppermute | solution.py:340
  37.0 4.9 %collective-permute-start.2 = (f32[64,128]{1,0:T(8,128)S(1)}, f32[64,128]{1,0:T(8,128)S(1)}, u32[]{:S(2)}, u32[]{:S(2)}) collective-permute-start(f32[64,128]{1,0:T(8,128)S(1)} %get-tuple-element.28), channel_id=1, source_target_pairs={{0,1},{1,0},{2,3},{3,2},{4,5},{5,4},{6,7},{7,6},{8,9},{9,8},{10,11... | collective-permute-start | bytes 98312 | tf_op jit(solution)/shard_map/ppermute | solution.py:339
  38.4 11.4 %collective-permute-start.3 = (f32[64,128]{1,0:T(8,128)S(1)}, f32[64,128]{1,0:T(8,128)S(1)}, u32[]{:S(2)}, u32[]{:S(2)}) collective-permute-start(f32[64,128]{1,0:T(8,128)S(1)} %get-tuple-element.29), channel_id=1, source_target_pairs={{0,7},{1,2},{2,1},{3,4},{4,3},{5,6},{6,5},{7,0},{8,15},{9,10},{10,... | collective-permute-start | bytes 98312 | tf_op jit(solution)/shard_map/ppermute | solution.py:340
  56.9 8.3 %collective-permute-start.4 = (f32[128,128]{1,0:T(8,128)S(1)}, f32[128,128]{1,0:T(8,128)S(1)}, u32[]{:S(2)}, u32[]{:S(2)}) collective-permute-start(f32[128,128]{1,0:T(8,128)S(1)} %get-tuple-element.32), channel_id=1, source_target_pairs={{0,8},{8,0},{16,24},{24,16},{1,9},{9,1},{17,25},{25,17},{2,10},{10... | collective-permute-start | bytes 196616 | tf_op jit(solution)/shard_map/ppermute | solution.py:339
  57.0 8.2 %collective-permute-start.5 = (f32[128,128]{1,0:T(8,128)S(1)}, f32[128,128]{1,0:T(8,128)S(1)}, u32[]{:S(2)}, u32[]{:S(2)}) collective-permute-start(f32[128,128]{1,0:T(8,128)S(1)} %get-tuple-element.33), channel_id=1, source_target_pairs={{0,24},{8,16},{16,8},{24,0},{1,25},{9,17},{17,9},{25,1},{2,26},{10... | collective-permute-start | bytes 196616 | tf_op jit(solution)/shard_map/ppermute | solution.py:340
  58.6 3.9 %collective-permute-start.6 = (f32[64,128]{1,0:T(8,128)S(1)}, f32[64,128]{1,0:T(8,128)S(1)}, u32[]{:S(2)}, u32[]{:S(2)}) collective-permute-start(f32[64,128]{1,0:T(8,128)S(1)} %get-tuple-element.34), channel_id=1, source_target_pairs={{0,1},{1,0},{2,3},{3,2},{4,5},{5,4},{6,7},{7,6},{8,9},{9,8},{10,11... | collective-permute-start | bytes 98312 | tf_op jit(solution)/shard_map/ppermute | solution.py:339
  58.6 6.6 %collective-permute-start.7 = (f32[64,128]{1,0:T(8,128)S(1)}, f32[64,128]{1,0:T(8,128)S(1)}, u32[]{:S(2)}, u32[]{:S(2)}) collective-permute-start(f32[64,128]{1,0:T(8,128)S(1)} %get-tuple-element.35), channel_id=1, source_target_pairs={{0,7},{1,2},{2,1},{3,4},{4,3},{5,6},{6,5},{7,0},{8,15},{9,10},{10,... | collective-permute-start | bytes 98312 | tf_op jit(solution)/shard_map/ppermute | solution.py:340
  65.2 7.5 %copy-start.2 = (s32[2048]{0:T(1024)S(1)}, s32[2048]{0:T(1024)}, u32[]{:S(2)}) copy-start(s32[2048]{0:T(1024)} %param.21) | copy-start | bytes 24580
  71.8 11.2 %collective-permute-start.8 = (f32[128,128]{1,0:T(8,128)S(1)}, f32[128,128]{1,0:T(8,128)S(1)}, u32[]{:S(2)}, u32[]{:S(2)}) collective-permute-start(f32[128,128]{1,0:T(8,128)S(1)} %get-tuple-element.37), channel_id=1, source_target_pairs={{0,8},{8,0},{16,24},{24,16},{1,9},{9,1},{17,25},{25,17},{2,10},{10... | collective-permute-start | bytes 196616 | tf_op jit(solution)/shard_map/ppermute | solution.py:339
  71.8 11.2 %collective-permute-start.9 = (f32[128,128]{1,0:T(8,128)S(1)}, f32[128,128]{1,0:T(8,128)S(1)}, u32[]{:S(2)}, u32[]{:S(2)}) collective-permute-start(f32[128,128]{1,0:T(8,128)S(1)} %get-tuple-element.38), channel_id=1, source_target_pairs={{0,24},{8,16},{16,8},{24,0},{1,25},{9,17},{17,9},{25,1},{2,26},{10... | collective-permute-start | bytes 196616 | tf_op jit(solution)/shard_map/ppermute | solution.py:340
  72.5 8.7 %collective-permute-start.10 = (f32[64,128]{1,0:T(8,128)S(1)}, f32[64,128]{1,0:T(8,128)S(1)}, u32[]{:S(2)}, u32[]{:S(2)}) collective-permute-start(f32[64,128]{1,0:T(8,128)S(1)} %get-tuple-element.39), channel_id=1, source_target_pairs={{0,1},{1,0},{2,3},{3,2},{4,5},{5,4},{6,7},{7,6},{8,9},{9,8},{10,11... | collective-permute-start | bytes 98312 | tf_op jit(solution)/shard_map/ppermute | solution.py:339
  74.8 1.6 %collective-permute-start.12 = (f32[8,256]{1,0:T(8,128)S(1)}, f32[8,256]{1,0:T(8,128)S(1)}, u32[]{:S(2)}, u32[]{:S(2)}) collective-permute-start(f32[8,256]{1,0:T(8,128)S(1)} %get-tuple-element.45), channel_id=1, source_target_pairs={{0,8},{8,0},{16,24},{24,16},{1,9},{9,1},{17,25},{25,17},{2,10},{10... | collective-permute-start | bytes 24584 | tf_op jit(solution)/shard_map/ppermute | solution.py:339
  74.8 3.3 %collective-permute-start.13 = (f32[8,256]{1,0:T(8,128)S(1)}, f32[8,256]{1,0:T(8,128)S(1)}, u32[]{:S(2)}, u32[]{:S(2)}) collective-permute-start(f32[8,256]{1,0:T(8,128)S(1)} %get-tuple-element.46), channel_id=1, source_target_pairs={{0,24},{8,16},{16,8},{24,0},{1,25},{9,17},{17,9},{25,1},{2,26},{10... | collective-permute-start | bytes 24584 | tf_op jit(solution)/shard_map/ppermute | solution.py:340
  76.4 6.6 %collective-permute-start.11 = (f32[64,128]{1,0:T(8,128)S(1)}, f32[64,128]{1,0:T(8,128)S(1)}, u32[]{:S(2)}, u32[]{:S(2)}) collective-permute-start(f32[64,128]{1,0:T(8,128)S(1)} %get-tuple-element.40), channel_id=1, source_target_pairs={{0,7},{1,2},{2,1},{3,4},{4,3},{5,6},{6,5},{7,0},{8,15},{9,10},{10,... | collective-permute-start | bytes 98312 | tf_op jit(solution)/shard_map/ppermute | solution.py:340
  78.1 11.0 %collective-permute-start.15 = (f32[64,128]{1,0:T(8,128)S(1)}, f32[64,128]{1,0:T(8,128)S(1)}, u32[]{:S(2)}, u32[]{:S(2)}) collective-permute-start(f32[64,128]{1,0:T(8,128)S(1)} %get-tuple-element.48), channel_id=1, source_target_pairs={{0,7},{1,2},{2,1},{3,4},{4,3},{5,6},{6,5},{7,0},{8,15},{9,10},{10,... | collective-permute-start | bytes 98312 | tf_op jit(solution)/shard_map/ppermute | solution.py:340
  81.2 7.9 %collective-permute-start.14 = (f32[64,128]{1,0:T(8,128)S(1)}, f32[64,128]{1,0:T(8,128)S(1)}, u32[]{:S(2)}, u32[]{:S(2)}) collective-permute-start(f32[64,128]{1,0:T(8,128)S(1)} %get-tuple-element.48), channel_id=1, source_target_pairs={{0,1},{1,0},{2,3},{3,2},{4,5},{5,4},{6,7},{7,6},{8,9},{9,8},{10,11... | collective-permute-start | bytes 98312 | tf_op jit(solution)/shard_map/ppermute | solution.py:339

commit v3 on v2

--- a/solution.py
+++ b/solution.py
@@ -1,4 +1,5 @@
 import functools
+from typing import NamedTuple
 
 import jax
 import jax.numpy as jnp
@@ -13,7 +14,8 @@
 SUB = 8
 LANES = 128
 PIECES = 4
-BULKS = 8
+BULKS = 4
+FIRST_BULKS = 2
 
 VMEM = pl.BlockSpec(memory_space=pltpu.VMEM)
 SMEM = pl.BlockSpec(memory_space=pltpu.SMEM)
@@ -107,10 +109,19 @@
     ]
     for copy in small:
         copy.start()
+    for b in range(loaded.shape[1]):
+        bulk_copies([(blocks_hbm, blocks_ref)], loaded, b)[0].start()
     for b in range(bulks):
         copies(b)[0].start()
-    for b in range(loaded.shape[1]):
-        bulk_copies([(blocks_hbm, blocks_ref)], loaded, b)[0].start()
+    for copy in small:
+        copy.wait()
+    owned, _, width = light.shape
+    for f in range(owned):
+        light[f] = emitted_ref[:, f * width : (f + 1) * width].astype(jnp.bfloat16)
+    finish = project(
+        light, blocks_ref, source_ref, live_ref, sent_hbm, sent_ref, done,
+        lambda b: bulk_copies([(blocks_hbm, blocks_ref)], loaded, b)[0].wait(),
+    )
 
     @pl.loop(0, bulks)
     def _(b):
@@ -122,15 +133,7 @@
 
     share_edges("gx", xa_ref, xb_ref, x_low, x_high)
     share_edges("gy", ya_ref, yb_ref, y_low, y_high)
-    for copy in small:
-        copy.wait()
-    owned, _, width = light.shape
-    for f in range(owned):
-        light[f] = emitted_ref[:, f * width : (f + 1) * width].astype(jnp.bfloat16)
-    project(
-        light, blocks_ref, source_ref, live_ref, sent_hbm, sent_ref, done,
-        lambda b: bulk_copies([(blocks_hbm, blocks_ref)], loaded, b)[0].wait(),
-    )
+    finish()
 
 
 def opening(q, emitted, blocks, source, live, message, light):
@@ -148,7 +151,7 @@
             pltpu.SMEM(live.shape, jnp.int32),
             light,
             pltpu.VMEM(message.shape, jnp.float32),
-            pltpu.SemaphoreType.DMA((1, BULKS)),
+            pltpu.SemaphoreType.DMA((1, FIRST_BULKS)),
             pltpu.SemaphoreType.DMA((1, PIECES)),
             pltpu.SemaphoreType.DMA((PIECES,)),
             pltpu.SemaphoreType.DMA((3,)),
@@ -166,25 +169,29 @@
     return jnp.abs(velocity) * ((far - 8.0 * near) + (2.0 * (back + ahead) + 3.0 * center))
 
 
-def stage_kernel(
-    coefficient, first_stage, last, begin, end, base_hbm, q_hbm, e_hbm, n_hbm, u_hbm,
-    xa_in, xb_in, ya_in, yb_in, *rest,
-):
-    if begin > 0:
-        _, *rest = rest
-    out_hbm, *rest = rest
-    if last:
-        if begin == 0:
-            ground_ref, *rest = rest
-    else:
-        xa_ref, xb_ref, ya_ref, yb_ref, *rest = rest
-    if first_stage:
-        speed_hbm, *rest = rest
-    x_low, x_high, y_low, y_high, padded, turned, base_ref, e_ref, n_ref, u_ref, out_ref, *rest = rest
-    speed_ref = n_ref
-    if first_stage:
-        speed_ref, *rest = rest
-    sems, done = rest
+def stage_kernel(coefficient, plan, *refs):
+    refs = list(refs)
+
+    def take(count, wanted=True):
+        return [refs.pop(0) for _ in range(count)] if wanted else [None] * count
+
+    (q_hbm,) = take(1)
+    (base_hbm,) = take(1, plan.own_base)
+    e_hbm, u_hbm = take(2, plan.xz)
+    (n_hbm,) = take(1, plan.y)
+    xa_in, xb_in = take(2, plan.xz)
+    ya_in, yb_in = take(2, plan.y)
+    (out_hbm,) = take(1)
+    xa_ref, xb_ref, ya_ref, yb_ref = take(4, plan.shares)
+    (speed_hbm,) = take(1, plan.turns)
+    (ground_ref,) = take(1, plan.ground)
+    padded, out_ref, sems, done = take(4)
+    x_low, x_high, y_low, y_high = take(4, plan.shares)
+    (base_ref,) = take(1, plan.own_base)
+    e_ref, u_ref = take(2, plan.xz)
+    turned, speed_ref = take(2, plan.y)
+    (n_ref,) = take(1, plan.turns)
+
     levels, rows, columns = out_ref.shape
     tiles = rows // SUB
     bulks = sems.shape[1]
@@ -195,72 +202,80 @@
         return bulk_copies([(q_hbm, padded)], sems, b)
 
     def others(b):
-        found = [(e_hbm, e_ref), (n_hbm, n_ref), (u_hbm, u_ref)]
-        if not first_stage:
+        found = []
+        if plan.xz:
+            found += [(e_hbm, e_ref), (u_hbm, u_ref)]
+        if plan.y:
+            found.append((n_hbm, n_ref if plan.turns else speed_ref))
+        if plan.own_base:
             found.append((base_hbm, base_ref))
-        return bulk_copies([(q_hbm, padded)] + found, sems, b)[1:]
+        return [
+            pltpu.make_async_copy(
+                source.at[pl.ds(b * (source.shape[0] // bulks), source.shape[0] // bulks)],
+                target.at[pl.ds(b * (source.shape[0] // bulks), source.shape[0] // bulks)],
+                sems.at[i + 1, b],
+            )
+            for i, (source, target) in enumerate(found)
+        ]
 
     def outgoing(b):
         found = [(out_ref, out_hbm)]
-        if first_stage:
+        if plan.turns:
             found.append((speed_ref, speed_hbm))
         return bulk_copies(found, done, b)
 
-    below, above = max(begin - 1, 0), min(end + 1, bulks)
-    for b in range(below, above):
+    for b in range(bulks):
         for copy in field(b):
             copy.start()
-    for b in range(begin, end):
+    for b in range(bulks):
         for copy in others(b):
             copy.start()
     even_x, even_y = is_even("gx"), is_even("gy")
 
-    @pl.loop(begin, end)
+    @pl.loop(0, bulks)
     def _(b):
         for copy in field(b):
             copy.wait()
         for i in range(count):
             p = b * count + i
-            for j in range(fold):
+            for j in range(fold if plan.xz else 0):
                 level = p * fold + j
                 at = edge_rows(b, count * fold, i * fold + j)
                 got_a, got_b = xa_in[at, :], xb_in[at, :]
                 padded[level, SUB - 2 : SUB, :] = jnp.where(even_x, got_b, got_a)
                 padded[level, SUB + rows : SUB + rows + 2, :] = jnp.where(even_x, got_a, got_b)
-            at = edge_rows(b, count, i)
-            got_a, got_b = ya_in[at, :], yb_in[at, :]
-            turned[p, SUB - 2 : SUB, :] = jnp.where(even_y, got_b, got_a)
-            turned[p, SUB + columns : SUB + columns + 2, :] = jnp.where(even_y, got_a, got_b)
-            q = padded[pl.ds(p * fold, fold), SUB : SUB + rows, :]
-            turned[p, SUB : SUB + columns, :] = q.reshape(fold * rows, columns).T
-
-    for b in [*range(below, begin), *range(end, above)]:
-        for copy in field(b):
-            copy.wait()
-
-    @pl.loop(begin, end)
+            if plan.y:
+                at = edge_rows(b, count, i)
+                got_a, got_b = ya_in[at, :], yb_in[at, :]
+                turned[p, SUB - 2 : SUB, :] = jnp.where(even_y, got_b, got_a)
+                turned[p, SUB + columns : SUB + columns + 2, :] = jnp.where(even_y, got_a, got_b)
+                q = padded[pl.ds(p * fold, fold), SUB : SUB + rows, :]
+                turned[p, SUB : SUB + columns, :] = q.reshape(fold * rows, columns).T
+
+    @pl.loop(0, bulks)
     def _(b):
         for copy in others(b):
             copy.wait()
         for i in range(count):
             p = b * count + i
-            if first_stage:
+            if plan.turns:
                 speed_ref[p] = n_ref[pl.ds(p * fold, fold)].reshape(fold * rows, columns).T
-            terms = []
-            for t in range(columns // SUB):
-
-                def line(offset):
-                    return turned[p, SUB + t * SUB + offset : 2 * SUB + t * SUB + offset, :]
-
-                terms.append(
-                    moved(line(-2), line(-1), line(0), line(1), line(2), speed_ref[p, t * SUB : (t + 1) * SUB, :])
-                )
-            along_y = jnp.concatenate(terms, axis=0).T
+            if plan.y:
+                terms = []
+                for t in range(columns // SUB):
+
+                    def line(offset):
+                        return turned[p, SUB + t * SUB + offset : 2 * SUB + t * SUB + offset, :]
+
+                    terms.append(
+                        moved(line(-2), line(-1), line(0), line(1), line(2), speed_ref[p, t * SUB : (t + 1) * SUB, :])
+                    )
+                along_y = jnp.concatenate(terms, axis=0).T
             results = [[] for _ in range(fold)]
             for t in range(tiles):
                 tile = slice(t * SUB, (t + 1) * SUB)
                 column = []
-                for d in range(-2, fold + 2):
+                for d in range(-2, fold + 2) if plan.xz else ():
                     level = p * fold + d
                     if i * fold + d < 0:
                         level = jnp.maximum(level, 0)
@@ -269,19 +284,22 @@
                     column.append(padded[level, SUB + t * SUB : 2 * SUB + t * SUB, :])
                 for j in range(fold):
                     level = p * fold + j
-
-                    def row(offset):
-                        return padded[level, SUB + t * SUB + offset : 2 * SUB + t * SUB + offset, :]
-
-                    q = column[j + 2]
-                    total = moved(row(-2), row(-1), q, row(1), row(2), e_ref[level, tile, :])
-                    total += moved(*column[j : j + 5], u_ref[level, tile, :])
-                    total += along_y[j * rows + t * SUB : j * rows + (t + 1) * SUB]
-                    base = q if first_stage else base_ref[level, tile, :]
+                    total = 0.0
+                    if plan.xz:
+
+                        def row(offset):
+                            return padded[level, SUB + t * SUB + offset : 2 * SUB + t * SUB + offset, :]
+
+                        q = column[j + 2]
+                        total = moved(row(-2), row(-1), q, row(1), row(2), e_ref[level, tile, :])
+                        total += moved(*column[j : j + 5], u_ref[level, tile, :])
+                    if plan.y:
+                        total += along_y[j * rows + t * SUB : j * rows + (t + 1) * SUB]
+                    base = base_ref[level, tile, :] if plan.own_base else q
                     result = base - (coefficient / 6.0) * total
                     out_ref[level, tile, :] = result
                     results[j].append(result)
-            if not last:
+            if plan.shares:
                 found = [jnp.concatenate(part, axis=0) for part in results]
                 keep_edges(
                     b, i, count, fold, found, jnp.concatenate(found, axis=0).T, x_low, x_high, y_low, y_high
@@ -289,50 +307,67 @@
         for copy in outgoing(b):
             copy.start()
 
-    if last:
-        if begin == 0:
-            ground_ref[...] = out_ref[0]
-    else:
+    if plan.ground:
+        ground_ref[...] = out_ref[0]
+    if plan.shares:
         share_edges("gx", xa_ref, xb_ref, x_low, x_high)
         share_edges("gy", ya_ref, yb_ref, y_low, y_high)
-    for b in range(begin, end):
+    for b in range(bulks):
         for copy in outgoing(b):
             copy.wait()
 
 
-def stage(base, q, winds, edges, coefficient, first_stage=False, last=False, begin=0, end=BULKS, started=None):
+class Plan(NamedTuple):
+    xz: bool = True
+    y: bool = True
+    own_base: bool = True
+    shares: bool = True
+    turns: bool = False
+    ground: bool = False
+
+
+def stage(plan, coefficient, q, base, winds_xz, wind_y, x_edges, y_edges):
     levels, rows, columns = q.shape
     blocks = levels * rows // LANES
-    whole = pltpu.HBM(q.shape, jnp.float32)
-    ground = jax.ShapeDtypeStruct((rows, columns), jnp.float32)
-    outs = (whole, *(() if last else edge_shapes(q.shape)))
-    outs += (ground,) if last and begin == 0 else ()
-    outs += (pltpu.HBM((blocks, columns, LANES), jnp.float32),) if first_stage else ()
     field = pltpu.VMEM(q.shape, jnp.float32)
     turned = pltpu.VMEM((blocks, columns, LANES), jnp.float32)
+    large, small = [q], []
+    outs = [pltpu.HBM(q.shape, jnp.float32)]
+    scratch = [
+        pltpu.VMEM((levels, rows + 2 * SUB, columns), jnp.float32),
+        field,
+        pltpu.SemaphoreType.DMA((5, BULKS)),
+        pltpu.SemaphoreType.DMA((2, BULKS)),
+    ]
+    if plan.shares:
+        outs += edge_shapes(q.shape)
+        scratch += edge_scratch(q.shape)
+    if plan.own_base:
+        large.append(base)
+        scratch.append(field)
+    if plan.xz:
+        large += winds_xz
+        small += x_edges
+        scratch += [field, field]
+    if plan.y:
+        large.append(wind_y)
+        small += y_edges
+        scratch += [pltpu.VMEM((blocks, columns + 2 * SUB, LANES), jnp.float32), turned]
+    if plan.turns:
+        outs.append(pltpu.HBM((blocks, columns, LANES), jnp.float32))
+        scratch.append(field)
+    if plan.ground:
+        outs.append(jax.ShapeDtypeStruct((rows, columns), jnp.float32))
     return pl.pallas_call(
-        functools.partial(stage_kernel, coefficient, first_stage, last, begin, end),
+        functools.partial(stage_kernel, coefficient, plan),
         out_shape=outs,
-        in_specs=[HBM] * 5 + [VMEM] * 4 + [HBM] * (begin > 0),
-        input_output_aliases={9: 0} if begin > 0 else {},
-        out_specs=tuple(HBM if isinstance(out, type(whole)) else VMEM for out in outs),
-        scratch_shapes=[
-            *edge_scratch(q.shape),
-            pltpu.VMEM((levels, rows + 2 * SUB, columns), jnp.float32),
-            pltpu.VMEM((blocks, columns + 2 * SUB, LANES), jnp.float32),
-            pltpu.VMEM((SUB, LANES), jnp.float32) if first_stage else field,
-            field,
-            field if first_stage else turned,
-            field,
-            field,
-            *([turned] if first_stage else []),
-            pltpu.SemaphoreType.DMA((5, BULKS)),
-            pltpu.SemaphoreType.DMA((2, BULKS)),
-        ],
+        in_specs=[HBM] * len(large) + [VMEM] * len(small),
+        out_specs=[HBM if isinstance(out, type(outs[0])) else VMEM for out in outs],
+        scratch_shapes=scratch,
         name="stage",
         compiler_params=grant(20),
-        cost_estimate=cost(24_000_000 * (end - begin) // BULKS, q.size * 24 * (end - begin) // BULKS),
-    )(*map(in_hbm, (base, q, *winds)), *edges, *([started] if begin > 0 else []))
+        cost_estimate=cost(24_000_000, q.size * 24),
+    )(*map(in_hbm, large), *small)
 
 
 def swap(array, axis):
@@ -344,7 +379,7 @@
 def neighbours(x_low, x_high, y_low, y_high):
     y_edges = swap((y_low, y_high), "gy")
     x_edges = swap((x_low, x_high), "gx")
-    return *x_edges, *y_edges
+    return x_edges, y_edges
 
 
 def exchange(sent):
@@ -381,8 +416,12 @@
                     sent_ref[r, c + d] = got[d * bands : (d + 1) * bands] * scale
 
         outgoing(p).start()
-    for p in range(pieces):
-        outgoing(p).wait()
+
+    def finish():
+        for p in range(pieces):
+            outgoing(p).wait()
+
+    return finish
 
 
 def gather_light(arrived_ref, target_ref, total):
@@ -414,7 +453,7 @@
     for f in range(blocks):
         at = slice(f * width, (f + 1) * width)
         light[f] = (emitted_ref[:, at] + albedo_ref[:, at] * total[f]).astype(jnp.bfloat16)
-    project(light, blocks_ref, source_ref, live_ref, sent_hbm, sent_ref, done, lambda p: incoming(p).wait())
+    project(light, blocks_ref, source_ref, live_ref, sent_hbm, sent_ref, done, lambda p: incoming(p).wait())()
 
 
 def last_kernel(
@@ -506,7 +545,6 @@
     message = pltpu.HBM((peers, slots, bands, width), jnp.float32)
     light = pltpu.VMEM((owned, bands, width), jnp.bfloat16)
     total = pltpu.VMEM((owned, bands, width), jnp.float32)
-    winds = (eastward_shift_ratio, northward_shift_ratio, upward_shift_ratio)
 
     *edges, sent = opening(
         thermal_anomaly, emitted_power, blocks, source, active_pairing_totals, message, light
@@ -514,8 +552,10 @@
     edges = neighbours(*edges)
     arrived = exchange(sent)
 
-    one, *sides, speed = stage(thermal_anomaly, thermal_anomaly, winds, edges, 1.0 / 3.0, first_stage=True)
-    winds = (eastward_shift_ratio, speed, upward_shift_ratio)
+    winds = (eastward_shift_ratio, upward_shift_ratio)
+    one, *sides, speed = stage(
+        Plan(own_base=False, turns=True), 1.0 / 3.0, thermal_anomaly, None, winds, northward_shift_ratio, *edges
+    )
     edges = neighbours(*sides)
 
     sent = pl.pallas_call(
@@ -537,8 +577,9 @@
     )(arrived, target, emitted_power, albedo_values, in_hbm(blocks), source, active_pairing_totals)
     arrived = exchange(sent)
 
-    two, *sides = stage(thermal_anomaly, one, winds, edges, 1.0 / 2.0)
+    two, *sides = stage(Plan(), 1.0 / 2.0, one, thermal_anomaly, winds, speed, *edges)
     edges = neighbours(*sides)
+    (part,) = stage(Plan(y=False, shares=False), 1.0, two, thermal_anomaly, winds, None, *edges)
 
     span_x = rows + 2 * MARGIN
     rim = jax.ShapeDtypeStruct((MARGIN, 2 * columns), jnp.float32)
@@ -563,7 +604,9 @@
     )(arrived, target, emitted_power, albedo_values, nearest_ground_index.reshape(owned, width))
     rims = swap(rims, "gx")
 
-    three, ground = stage(thermal_anomaly, two, winds, edges, 1.0, last=True)
+    three, ground = stage(
+        Plan(xz=False, shares=False, ground=True), 1.0, two, part, None, speed, *edges
+    )
 
     flat = jax.ShapeDtypeStruct((rows, columns), jnp.float32)
     middle, side = pl.pallas_call(

time: 90.1 us -> 89.5 us (level)
  the two profiles are of different devices: /device:TPU:0 before, /device:TPU:1 now
where the time goes in v3:
time: 89.5 us; the launch traced here: 87.9 us
  Pallas kernels  31.7 us (35%)
  blocking collectives  22.8 us (25%)
  starting transfers between devices  19 us (21%)
  waiting for transfers between devices  13.6 us (15%)
    all_to_all x1, blocking collectives, exchange(): lax.all_to_all(sent, ('gx', 'gy'), split_axis=0, concat_axis=0, tiled=True)  22.8 us
    pallas_call x4, Pallas kernels, stage(): pl.pallas_call(functools.partial(stage_kernel, coefficient, plan), out_sh...  21.9 us
    ppermute x8, starting transfers between devices, swap(): b = lax.ppermute(array[1], axis, swap_high(axis))  10.9 us
    ppermute x8, waiting for transfers between devices, swap(): b = lax.ppermute(array[1], axis, swap_high(axis))  10.9 us
    ppermute x8, starting transfers between devices, swap(): a = lax.ppermute(array[0], axis, swap_low(axis))  5.07 us
    pallas_call x1, Pallas kernels, step(): pl.pallas_call(second_kernel, out_shape=message, in_specs=[VMEM, SMEM, VM...  3.69 us
    pallas_call x1, Pallas kernels, opening(): pl.pallas_call(opening_kernel, out_shape=(*edge_shapes(q.shape), message)...  3.39 us
    all_to_all x1, starting transfers between devices, exchange(): lax.all_to_all(sent, ('gx', 'gy'), split_axis=0, concat_axis=0, tiled=True)  2.98 us
  transfers between devices with their start and end apart: 17, of which 4 were waited for; matrix products, arithmetic and copies ran while one was open for 0% of the time, Pallas kernels for 27%

profile of v3, /device:TPU:1, one launch (start us, length us, event | category | flops | bytes accessed | tf_op | source)
XLA Modules:
  0.0 87.9 jit_solution(10229113991244589468)
XLA Ops:
  0.7 3.4 %opening.1 = (f32[128,128]{1,0:T(8,128)S(1)}, f32[128,128]{1,0:T(8,128)S(1)}, f32[64,128]{1,0:T(8,128)S(1)}, f32[64,128]{1,0:T(8,128)S(1)}, f32[32,2,16,128]{3,2,1,0:T(8,128)}) custom-call(f32[64,64,128]{2,1,0:T(8,128)} %refs_1_.5, f32[16,2048]{1,0:T(8,128)} %emitted_ref.3, bf16[32,2,128,128]{3,2,1,0:T(8,128)(2,1)} %bitcast.13, s32[2,32]{1,0:T(2,128)} %bitcast.9, ...), custom_call_target="tpu_custom_call" | custom-call | flops 12000000 | bytes 4194304 | tf_op jit(solution)/shard_map/opening/pallas_call | solution.py:140
  4.1 22.8 %all_to_all.10.arrived_ref = f32[32,2,16,128]{3,2,1,0:T(8,128)S(1)} all-to-all(f32[32,2,16,128]{3,2,1,0:T(8,128)} %get-tuple-element.43), channel_id=1, replica_groups=mesh['gx'=4,'gy'=8] {'gx','gy'}, dimensions={0} | all-to-all | bytes 1048576 | tf_op jit(solution)/shard_map/all_to_all | solution.py:386
  26.9 3.7 %second.1 = f32[32,2,16,128]{3,2,1,0:T(8,128)} custom-call(f32[32,2,16,128]{3,2,1,0:T(8,128)S(1)} %all_to_all.10.arrived_ref, s32[2,32]{1,0:T(2,128)S(1)} %bitcast.11, f32[16,2048]{1,0:T(8,128)S(1)} %copy-done, f32[16,2048]{1,0:T(8,128)S(1)} %copy-done.1, bf16[32,2,128,128]{3,2,1,0:T(8,128)(2,1)} %bitcast.14, s32[2,32]{1,0:T(2,128)S(1)} %bitcast.10, ...), custom_call_target="tpu_custom_call" | custom-call | flops 12000000 | bytes 2097152 | tf_op jit(solution)/shard_map/second/pallas_call | solution.py:561
  30.6 3.0 %all-to-all-start.1 = ((f32[32,2,16,128]{3,2,1,0:T(8,128)}), f32[32,2,16,128]{3,2,1,0:T(8,128)S(1)}, u32[]{:S(2)}, u32[]{:S(2)}) async-start(f32[32,2,16,128]{3,2,1,0:T(8,128)} %second.1), calls=%async_computation.1 | async-start | bytes 1048576 | tf_op jit(solution)/shard_map/all_to_all | solution.py:386
  33.6 0.5 collective-permute-start
  34.1 1.4 %collective-permute-start.1 = (f32[128,128]{1,0:T(8,128)S(1)}, f32[128,128]{1,0:T(8,128)S(1)}, u32[]{:S(2)}, u32[]{:S(2)}) collective-permute-start(f32[128,128]{1,0:T(8,128)S(1)} %get-tuple-element.27), channel_id=1, source_target_pairs={{0,24},{8,16},{16,8},{24,0},{1,25},{9,17},{17,9},{25,1},{2,26},{10... | collective-permute-start | bytes 196616 | tf_op jit(solution)/shard_map/ppermute | solution.py:375
  35.5 1.2 %collective-permute-start.2 = (f32[64,128]{1,0:T(8,128)S(1)}, f32[64,128]{1,0:T(8,128)S(1)}, u32[]{:S(2)}, u32[]{:S(2)}) collective-permute-start(f32[64,128]{1,0:T(8,128)S(1)} %get-tuple-element.28), channel_id=1, source_target_pairs={{0,1},{1,0},{2,3},{3,2},{4,5},{5,4},{6,7},{7,6},{8,9},{9,8},{10,11... | collective-permute-start | bytes 98312 | tf_op jit(solution)/shard_map/ppermute | solution.py:374
  36.7 3.2 %collective-permute-start.3 = (f32[64,128]{1,0:T(8,128)S(1)}, f32[64,128]{1,0:T(8,128)S(1)}, u32[]{:S(2)}, u32[]{:S(2)}) collective-permute-start(f32[64,128]{1,0:T(8,128)S(1)} %get-tuple-element.29), channel_id=1, source_target_pairs={{0,7},{1,2},{2,1},{3,4},{4,3},{5,6},{6,5},{7,0},{8,15},{9,10},{10,... | collective-permute-start | bytes 98312 | tf_op jit(solution)/shard_map/ppermute | solution.py:375
  39.9 7.7 %collective-permute-done.3.refs_7_ = f32[64,128]{1,0:T(8,128)S(1)} collective-permute-done((f32[64,128]{1,0:T(8,128)S(1)}, f32[64,128]{1,0:T(8,128)S(1)}, u32[]{:S(2)}, u32[]{:S(2)}) %collective-permute-start.3) | collective-permute-done | bytes 32800 | tf_op jit(solution)/shard_map/ppermute | solution.py:375
  47.5 6.8 %stage.4 = (f32[64,64,128]{2,1,0:T(8,128)}, f32[128,128]{1,0:T(8,128)S(1)}, f32[128,128]{1,0:T(8,128)S(1)}, f32[64,128]{1,0:T(8,128)S(1)}, f32[64,128]{1,0:T(8,128)S(1)}, /*index=5*/f32[32,128,128]{2,1,0:T(8,128)}) custom-call(f32[64,64,128]{2,1,0:T(8,128)} %refs_1_.5, f32[64,64,128]{2,1,0:T(8,128)} %refs_2_.5, f32[64,64,128]{2,1,0:T(8,128)} %refs_3_.5, ...), custom_call_target="tpu_custom_call" | custom-call | flops 24000000 | bytes 12582912 | tf_op jit(solution)/shard_map/stage/pallas_call | solution.py:361
  54.3 1.3 %collective-permute-start.4 = (f32[128,128]{1,0:T(8,128)S(1)}, f32[128,128]{1,0:T(8,128)S(1)}, u32[]{:S(2)}, u32[]{:S(2)}) collective-permute-start(f32[128,128]{1,0:T(8,128)S(1)} %get-tuple-element.32), channel_id=1, source_target_pairs={{0,8},{8,0},{16,24},{24,16},{1,9},{9,1},{17,25},{25,17},{2,10},{10... | collective-permute-start | bytes 196616 | tf_op jit(solution)/shard_map/ppermute | solution.py:374
  55.6 1.2 %collective-permute-start.5 = (f32[128,128]{1,0:T(8,128)S(1)}, f32[128,128]{1,0:T(8,128)S(1)}, u32[]{:S(2)}, u32[]{:S(2)}) collective-permute-start(f32[128,128]{1,0:T(8,128)S(1)} %get-tuple-element.33), channel_id=1, source_target_pairs={{0,24},{8,16},{16,8},{24,0},{1,25},{9,17},{17,9},{25,1},{2,26},{10... | collective-permute-start | bytes 196616 | tf_op jit(solution)/shard_map/ppermute | solution.py:375
  56.9 2.7 %collective-permute-done.6.refs_7_ = f32[64,128]{1,0:T(8,128)S(1)} collective-permute-done((f32[64,128]{1,0:T(8,128)S(1)}, f32[64,128]{1,0:T(8,128)S(1)}, u32[]{:S(2)}, u32[]{:S(2)}) %collective-permute-start.6) | collective-permute-done | bytes 32800 | tf_op jit(solution)/shard_map/ppermute | solution.py:374
  59.6 2.7 %collective-permute-done.7.refs_8_ = f32[64,128]{1,0:T(8,128)S(1)} collective-permute-done((f32[64,128]{1,0:T(8,128)S(1)}, f32[64,128]{1,0:T(8,128)S(1)}, u32[]{:S(2)}, u32[]{:S(2)}) %collective-permute-start.7) | collective-permute-done | bytes 32800 | tf_op jit(solution)/shard_map/ppermute | solution.py:375
  62.3 6.1 %stage.5 = (f32[64,64,128]{2,1,0:T(8,128)}, f32[128,128]{1,0:T(8,128)S(1)}, f32[128,128]{1,0:T(8,128)S(1)}, f32[64,128]{1,0:T(8,128)S(1)}, f32[64,128]{1,0:T(8,128)S(1)}) custom-call(f32[64,64,128]{2,1,0:T(8,128)} %get-tuple-element.30.refs_0_, f32[64,64,128]{2,1,0:T(8,128)} %refs_1_.5, f32[64,64,128]{2,1,0:T(8,128)} %refs_2_.5, f32[64,64,128]{2,1,0:T(8,128)} %refs_3_.5, ...), custom_call_target="tpu_custom_call" | custom-call | flops 24000000 | bytes 12582912 | tf_op jit(solution)/shard_map/stage/pallas_call | solution.py:361
  68.4 1.6 %collective-permute-start.8 = (f32[128,128]{1,0:T(8,128)S(1)}, f32[128,128]{1,0:T(8,128)S(1)}, u32[]{:S(2)}, u32[]{:S(2)}) collective-permute-start(f32[128,128]{1,0:T(8,128)S(1)} %get-tuple-element.37), channel_id=1, source_target_pairs={{0,8},{8,0},{16,24},{24,16},{1,9},{9,1},{17,25},{25,17},{2,10},{10... | collective-permute-start | bytes 196616 | tf_op jit(solution)/shard_map/ppermute | solution.py:374
  70.3 2.1 %last.1 = (f32[16,2048]{1,0:T(8,128)}, f32[64,256]{1,0:T(8,128)S(1)}, f32[8,256]{1,0:T(8,128)S(1)}, f32[8,256]{1,0:T(8,128)S(1)}) custom-call(f32[32,2,16,128]{3,2,1,0:T(8,128)S(1)} %all-to-all-done.1.arrived_ref, s32[2,32]{1,0:T(2,128)S(1)} %bitcast.12, f32[16,2048]{1,0:T(8,128)S(1)} %copy-done, f32[16,2048]{1,0:T(8,128)S(1)} %copy-done.1, ...), custom_call_target="tpu_custom_call" | custom-call | flops 16000000 | bytes 524288 | tf_op jit(solution)/shard_map/last/pallas_call | solution.py:586
  72.8 1.2 %collective-permute-start.13 = (f32[8,256]{1,0:T(8,128)S(1)}, f32[8,256]{1,0:T(8,128)S(1)}, u32[]{:S(2)}, u32[]{:S(2)}) collective-permute-start(f32[8,256]{1,0:T(8,128)S(1)} %get-tuple-element.46), channel_id=1, source_target_pairs={{0,24},{8,16},{16,8},{24,0},{1,25},{9,17},{17,9},{25,1},{2,26},{10... | collective-permute-start | bytes 24584 | tf_op jit(solution)/shard_map/ppermute | solution.py:375
  73.9 1.4 %collective-permute-start.11 = (f32[64,128]{1,0:T(8,128)S(1)}, f32[64,128]{1,0:T(8,128)S(1)}, u32[]{:S(2)}, u32[]{:S(2)}) collective-permute-start(f32[64,128]{1,0:T(8,128)S(1)} %get-tuple-element.40), channel_id=1, source_target_pairs={{0,7},{1,2},{2,1},{3,4},{4,3},{5,6},{6,5},{7,0},{8,15},{9,10},{10,... | collective-permute-start | bytes 98312 | tf_op jit(solution)/shard_map/ppermute | solution.py:375
  75.3 0.5 collective-permute-done.13.rim_b_ref
  75.8 2.4 %collective-permute-start.15 = (f32[64,128]{1,0:T(8,128)S(1)}, f32[64,128]{1,0:T(8,128)S(1)}, u32[]{:S(2)}, u32[]{:S(2)}) collective-permute-start(f32[64,128]{1,0:T(8,128)S(1)} %get-tuple-element.48), channel_id=1, source_target_pairs={{0,7},{1,2},{2,1},{3,4},{4,3},{5,6},{6,5},{7,0},{8,15},{9,10},{10,... | collective-permute-start | bytes 98312 | tf_op jit(solution)/shard_map/ppermute | solution.py:375
  78.2 4.9 %stage.6.refs_1_ = f32[64,64,128]{2,1,0:T(8,128)} custom-call(f32[64,64,128]{2,1,0:T(8,128)} %get-tuple-element.36.refs_0_, f32[64,64,128]{2,1,0:T(8,128)} %refs_1_.5, f32[64,64,128]{2,1,0:T(8,128)} %refs_2_.5, f32[64,64,128]{2,1,0:T(8,128)} %refs_3_.5, f32[128,128]{1,0:T(8,128)S(1)} %collective-permute-done.8.refs_4_, ...), custom_call_target="tpu_custom_call" | custom-call | flops 24000000 | bytes 12582912 | tf_op jit(solution)/shard_map/stage/pallas_call | solution.py:361
  83.2 4.1 %stage.7 = (f32[64,64,128]{2,1,0:T(8,128)}, f32[64,128]{1,0:T(8,128)S(1)}) custom-call(f32[64,64,128]{2,1,0:T(8,128)} %get-tuple-element.36.refs_0_, f32[64,64,128]{2,1,0:T(8,128)} %stage.6.refs_1_, f32[32,128,128]{2,1,0:T(8,128)} %get-tuple-element.31.refs_4_.refs_2_, f32[64,128]{1,0:T(8,128)S(1)} %collective-permute-done.10.refs_3_, ...), custom_call_target="tpu_custom_call" | custom-call | flops 24000000 | bytes 12582912 | tf_op jit(solution)/shard_map/stage/pallas_call | solution.py:361
  87.3 0.6 finish.1
  (32 shorter events, 0.8 us)
Async XLA Ops:
  0.6 26.3 %copy-start = (f32[16,2048]{1,0:T(8,128)S(1)}, f32[16,2048]{1,0:T(8,128)}, u32[]{:S(2)}) copy-start(f32[16,2048]{1,0:T(8,128)} %emitted_ref.3) | copy-start | bytes 393220
  0.6 26.3 %copy-start.1 = (f32[16,2048]{1,0:T(8,128)S(1)}, f32[16,2048]{1,0:T(8,128)}, u32[]{:S(2)}) copy-start(f32[16,2048]{1,0:T(8,128)} %albedo_ref.3) | copy-start | bytes 393220
  0.7 26.3 %copy-start.3 = (s32[1,32,2]{1,2,0:T(2,128)S(1)}, s32[1,32,2]{1,2,0:T(2,128)}, u32[]{:S(2)}) copy-start(s32[1,32,2]{1,2,0:T(2,128)} %param.19) | copy-start | bytes 772
  0.7 26.3 %copy-start.4 = (s32[32,1,2]{0,2,1:T(2,128)S(1)}, s32[32,1,2]{0,2,1:T(2,128)}, u32[]{:S(2)}) copy-start(s32[32,1,2]{0,2,1:T(2,128)} %param.20) | copy-start | bytes 772
  0.7 26.3 %copy-start.5 = (s32[1,32]{1,0:T(1,128)S(1)}, s32[1,32]{1,0:T(1,128)}, u32[]{:S(2)}) copy-start(s32[1,32]{1,0:T(1,128)} %live_ref.1) | copy-start | bytes 388
  30.6 39.6 %all-to-all-start.1 = ((f32[32,2,16,128]{3,2,1,0:T(8,128)}), f32[32,2,16,128]{3,2,1,0:T(8,128)S(1)}, u32[]{:S(2)}, u32[]{:S(2)}) async-start(f32[32,2,16,128]{3,2,1,0:T(8,128)} %second.1), calls=%async_computation.1 | async-start | bytes 1048576 | tf_op jit(solution)/shard_map/all_to_all | solution.py:386
  33.6 13.9 %collective-permute-start = (f32[128,128]{1,0:T(8,128)S(1)}, f32[128,128]{1,0:T(8,128)S(1)}, u32[]{:S(2)}, u32[]{:S(2)}) collective-permute-start(f32[128,128]{1,0:T(8,128)S(1)} %get-tuple-element.26), channel_id=1, source_target_pairs={{0,8},{8,0},{16,24},{24,16},{1,9},{9,1},{17,25},{25,17},{2,10},{10... | collective-permute-start | bytes 196616 | tf_op jit(solution)/shard_map/ppermute | solution.py:374
  34.1 13.4 %collective-permute-start.1 = (f32[128,128]{1,0:T(8,128)S(1)}, f32[128,128]{1,0:T(8,128)S(1)}, u32[]{:S(2)}, u32[]{:S(2)}) collective-permute-start(f32[128,128]{1,0:T(8,128)S(1)} %get-tuple-element.27), channel_id=1, source_target_pairs={{0,24},{8,16},{16,8},{24,0},{1,25},{9,17},{17,9},{25,1},{2,26},{10... | collective-permute-start | bytes 196616 | tf_op jit(solution)/shard_map/ppermute | solution.py:375
  35.5 4.4 %collective-permute-start.2 = (f32[64,128]{1,0:T(8,128)S(1)}, f32[64,128]{1,0:T(8,128)S(1)}, u32[]{:S(2)}, u32[]{:S(2)}) collective-permute-start(f32[64,128]{1,0:T(8,128)S(1)} %get-tuple-element.28), channel_id=1, source_target_pairs={{0,1},{1,0},{2,3},{3,2},{4,5},{5,4},{6,7},{7,6},{8,9},{9,8},{10,11... | collective-permute-start | bytes 98312 | tf_op jit(solution)/shard_map/ppermute | solution.py:374
  36.7 10.8 %collective-permute-start.3 = (f32[64,128]{1,0:T(8,128)S(1)}, f32[64,128]{1,0:T(8,128)S(1)}, u32[]{:S(2)}, u32[]{:S(2)}) collective-permute-start(f32[64,128]{1,0:T(8,128)S(1)} %get-tuple-element.29), channel_id=1, source_target_pairs={{0,7},{1,2},{2,1},{3,4},{4,3},{5,6},{6,5},{7,0},{8,15},{9,10},{10,... | collective-permute-start | bytes 98312 | tf_op jit(solution)/shard_map/ppermute | solution.py:375
  54.3 8.0 %collective-permute-start.4 = (f32[128,128]{1,0:T(8,128)S(1)}, f32[128,128]{1,0:T(8,128)S(1)}, u32[]{:S(2)}, u32[]{:S(2)}) collective-permute-start(f32[128,128]{1,0:T(8,128)S(1)} %get-tuple-element.32), channel_id=1, source_target_pairs={{0,8},{8,0},{16,24},{24,16},{1,9},{9,1},{17,25},{25,17},{2,10},{10... | collective-permute-start | bytes 196616 | tf_op jit(solution)/shard_map/ppermute | solution.py:374
  55.6 6.7 %collective-permute-start.5 = (f32[128,128]{1,0:T(8,128)S(1)}, f32[128,128]{1,0:T(8,128)S(1)}, u32[]{:S(2)}, u32[]{:S(2)}) collective-permute-start(f32[128,128]{1,0:T(8,128)S(1)} %get-tuple-element.33), channel_id=1, source_target_pairs={{0,24},{8,16},{16,8},{24,0},{1,25},{9,17},{17,9},{25,1},{2,26},{10... | collective-permute-start | bytes 196616 | tf_op jit(solution)/shard_map/ppermute | solution.py:375
  56.8 2.8 %collective-permute-start.6 = (f32[64,128]{1,0:T(8,128)S(1)}, f32[64,128]{1,0:T(8,128)S(1)}, u32[]{:S(2)}, u32[]{:S(2)}) collective-permute-start(f32[64,128]{1,0:T(8,128)S(1)} %get-tuple-element.34), channel_id=1, source_target_pairs={{0,1},{1,0},{2,3},{3,2},{4,5},{5,4},{6,7},{7,6},{8,9},{9,8},{10,11... | collective-permute-start | bytes 98312 | tf_op jit(solution)/shard_map/ppermute | solution.py:374
  56.8 5.5 %collective-permute-start.7 = (f32[64,128]{1,0:T(8,128)S(1)}, f32[64,128]{1,0:T(8,128)S(1)}, u32[]{:S(2)}, u32[]{:S(2)}) collective-permute-start(f32[64,128]{1,0:T(8,128)S(1)} %get-tuple-element.35), channel_id=1, source_target_pairs={{0,7},{1,2},{2,1},{3,4},{4,3},{5,6},{6,5},{7,0},{8,15},{9,10},{10,... | collective-permute-start | bytes 98312 | tf_op jit(solution)/shard_map/ppermute | solution.py:375
  62.3 8.0 %copy-start.2 = (s32[2048]{0:T(1024)S(1)}, s32[2048]{0:T(1024)}, u32[]{:S(2)}) copy-start(s32[2048]{0:T(1024)} %param.21) | copy-start | bytes 24580
  68.4 9.8 %collective-permute-start.8 = (f32[128,128]{1,0:T(8,128)S(1)}, f32[128,128]{1,0:T(8,128)S(1)}, u32[]{:S(2)}, u32[]{:S(2)}) collective-permute-start(f32[128,128]{1,0:T(8,128)S(1)} %get-tuple-element.37), channel_id=1, source_target_pairs={{0,8},{8,0},{16,24},{24,16},{1,9},{9,1},{17,25},{25,17},{2,10},{10... | collective-permute-start | bytes 196616 | tf_op jit(solution)/shard_map/ppermute | solution.py:374
  70.0 8.2 %collective-permute-start.9 = (f32[128,128]{1,0:T(8,128)S(1)}, f32[128,128]{1,0:T(8,128)S(1)}, u32[]{:S(2)}, u32[]{:S(2)}) collective-permute-start(f32[128,128]{1,0:T(8,128)S(1)} %get-tuple-element.38), channel_id=1, source_target_pairs={{0,24},{8,16},{16,8},{24,0},{1,25},{9,17},{17,9},{25,1},{2,26},{10... | collective-permute-start | bytes 196616 | tf_op jit(solution)/shard_map/ppermute | solution.py:375
  72.3 1.6 %collective-permute-start.12 = (f32[8,256]{1,0:T(8,128)S(1)}, f32[8,256]{1,0:T(8,128)S(1)}, u32[]{:S(2)}, u32[]{:S(2)}) collective-permute-start(f32[8,256]{1,0:T(8,128)S(1)} %get-tuple-element.45), channel_id=1, source_target_pairs={{0,8},{8,0},{16,24},{24,16},{1,9},{9,1},{17,25},{25,17},{2,10},{10... | collective-permute-start | bytes 24584 | tf_op jit(solution)/shard_map/ppermute | solution.py:374
  72.8 3.1 %collective-permute-start.13 = (f32[8,256]{1,0:T(8,128)S(1)}, f32[8,256]{1,0:T(8,128)S(1)}, u32[]{:S(2)}, u32[]{:S(2)}) collective-permute-start(f32[8,256]{1,0:T(8,128)S(1)} %get-tuple-element.46), channel_id=1, source_target_pairs={{0,24},{8,16},{16,8},{24,0},{1,25},{9,17},{17,9},{25,1},{2,26},{10... | collective-permute-start | bytes 24584 | tf_op jit(solution)/shard_map/ppermute | solution.py:375
  73.9 9.2 %collective-permute-start.10 = (f32[64,128]{1,0:T(8,128)S(1)}, f32[64,128]{1,0:T(8,128)S(1)}, u32[]{:S(2)}, u32[]{:S(2)}) collective-permute-start(f32[64,128]{1,0:T(8,128)S(1)} %get-tuple-element.39), channel_id=1, source_target_pairs={{0,1},{1,0},{2,3},{3,2},{4,5},{5,4},{6,7},{7,6},{8,9},{9,8},{10,11... | collective-permute-start | bytes 98312 | tf_op jit(solution)/shard_map/ppermute | solution.py:374
  73.9 9.2 %collective-permute-start.11 = (f32[64,128]{1,0:T(8,128)S(1)}, f32[64,128]{1,0:T(8,128)S(1)}, u32[]{:S(2)}, u32[]{:S(2)}) collective-permute-start(f32[64,128]{1,0:T(8,128)S(1)} %get-tuple-element.40), channel_id=1, source_target_pairs={{0,7},{1,2},{2,1},{3,4},{4,3},{5,6},{6,5},{7,0},{8,15},{9,10},{10,... | collective-permute-start | bytes 98312 | tf_op jit(solution)/shard_map/ppermute | solution.py:375
  75.8 11.4 %collective-permute-start.15 = (f32[64,128]{1,0:T(8,128)S(1)}, f32[64,128]{1,0:T(8,128)S(1)}, u32[]{:S(2)}, u32[]{:S(2)}) collective-permute-start(f32[64,128]{1,0:T(8,128)S(1)} %get-tuple-element.48), channel_id=1, source_target_pairs={{0,7},{1,2},{2,1},{3,4},{4,3},{5,6},{6,5},{7,0},{8,15},{9,10},{10,... | collective-permute-start | bytes 98312 | tf_op jit(solution)/shard_map/ppermute | solution.py:375
  78.2 9.1 %collective-permute-start.14 = (f32[64,128]{1,0:T(8,128)S(1)}, f32[64,128]{1,0:T(8,128)S(1)}, u32[]{:S(2)}, u32[]{:S(2)}) collective-permute-start(f32[64,128]{1,0:T(8,128)S(1)} %get-tuple-element.48), channel_id=1, source_target_pairs={{0,1},{1,0},{2,3},{3,2},{4,5},{5,4},{6,7},{7,6},{8,9},{9,8},{10,11... | collective-permute-start | bytes 98312 | tf_op jit(solution)/shard_map/ppermute | solution.py:374
